TPU v7x, 256 devices: a whole 4x4x8 slice. The times are simulated.
256 devices in a mesh: blk: 32 (over y, z), tile: 8 (over x, core).
Axes of the slice: x: 4, y: 4, z: 8, core: 2. Of those that a mesh axis runs over, the one named last changes fastest.
Arguments:
- anomalies: bfloat16 [256, 2048, 128], P('blk', 'tile'), may hold values from -40 to 40
- predecessors: int32 [256, 4], P('blk'), may hold values from 0 to 255, as said below
Outputs:
- precision_applied: float32 [256, 2048, 128], P('blk', 'tile')
- coefficients: bfloat16 [256, 512, 128], P(('blk', 'tile'))
- variances: float32 [256, 128], P('blk')
Inputs may be any that keep to these rules, and one draw needn't show every extreme that they name: predecessors[k, j] = (k - o) mod 256, with offsets o that differ within a row and lie in 1 to 32.
All inputs are finite; a program needn't handle non-finite values.
Results may differ from a plain program's by a relative error of at most 0.006.
Values may be sent and summed in bfloat16 or wider, within the bound.
A program may use at most 128 MiB of HBM per device.

v0:
```python
import jax
import jax.numpy as jnp
from jax import lax
from jax.sharding import Mesh
from jax.sharding import PartitionSpec as P

TILE = ("tile_0", "tile_1")
BLK_TILE = ("blk", "tile_0", "tile_1")


RIDGE_TERM = 0.25
EPSILON = 1e-05


def from_behind(block, axis, distance):
    devices = range(lax.axis_size(axis))
    route = [((i - distance) % len(devices), i) for i in devices]
    return lax.ppermute(block, axis, route)


def split_up(value, dim, peers):
    dims = value.shape
    tiles = value.reshape(*dims[:dim], peers, dims[dim] // peers, *dims[dim + 1 :])
    return jnp.moveaxis(tiles, dim, 0)


def in_order(tiles, dim):
    dims = list(tiles.shape[1:])
    dims[dim] *= tiles.shape[0]
    return jnp.moveaxis(tiles, 0, dim).reshape(dims)


def moved_by_axis(tiles, axes, order):
    dims = [lax.axis_size(a) for a in axes]
    tiles = tiles.reshape(*dims, *tiles.shape[1:])
    for k in order:
        tiles = lax.all_to_all(tiles, axes[k], split_axis=k, concat_axis=k, tiled=True)
    return tiles.reshape(-1, *tiles.shape[len(axes) :])


def exchange_by_chip(value, groups, order, split_dim, concat_dim):
    peers = lax.axis_size(groups[0]) * lax.axis_size(groups[1])
    tiles = split_up(value, split_dim, peers)
    return in_order(moved_by_axis(tiles, groups, order), concat_dim)


def copy_for_each(value, axis):
    peers = lax.axis_size(axis)
    return lax.all_to_all(
        jnp.broadcast_to(value[None], (peers, *value.shape)), axis, 0, 0, tiled=True
    )


def gather_directly(value, axis, dim):
    tiles = copy_for_each(value, axis)
    return in_order(tiles, dim)


def taken_together(value, axis):
    return copy_for_each(value, axis).sum(axis=0)


def solve_blocks(summed, block_rows):
    pred_rows = 4 * block_rows
    gram_part = summed[:, :, :pred_rows] + RIDGE_TERM * jnp.eye(pred_rows, dtype=jnp.float32)
    target = summed[:, :, pred_rows:]
    factor = jnp.linalg.cholesky(gram_part)
    middle = lax.linalg.triangular_solve(factor, target, left_side=True, lower=True)
    return lax.linalg.triangular_solve(factor, middle, left_side=True, lower=True, transpose_a=True)


def products(picked, own_blocks, members):
    amount = own_blocks.shape[0]
    block_rows = own_blocks.shape[2]
    gram_part = jnp.einsum("bjmr,bimq->bjriq", picked, picked, preferred_element_type=jnp.float32)
    gram_part = gram_part.reshape(amount, 4 * block_rows, 4 * block_rows)
    cross_part = jnp.einsum(
        "bjmr,bmq->bjrq", picked, own_blocks, preferred_element_type=jnp.float32
    )
    cross_part = cross_part.reshape(amount, 4 * block_rows, block_rows)
    return jnp.concatenate([gram_part, cross_part], axis=2) / members


def local(anomalies, predecessors):
    blocks = anomalies.shape[0]
    block_rows = anomalies.shape[2]
    position = lax.axis_index("blk")
    total_blocks = blocks * lax.axis_size("blk")
    members = anomalies.shape[1] * lax.axis_size(TILE)
    pieces = []
    for offset in range(4, 0, -1):
        pieces.append(from_behind(anomalies, "blk", offset))
    window = jnp.concatenate(pieces + [anomalies], axis=0)
    window_start = (position - 4) * blocks
    local_index = jnp.mod(predecessors - window_start, total_blocks)
    picked = jnp.take(window, local_index, axis=0)
    stacked = jnp.concatenate([picked, anomalies[:, None]], axis=1)
    exchanged = exchange_by_chip(stacked, ("tile_0", "tile_1"), (1, 0), 0, 2)
    summed = products(exchanged[:, :4], exchanged[:, 4], members)
    coefficients = solve_blocks(summed, block_rows).astype(jnp.bfloat16)
    gathered = gather_directly(coefficients, TILE, 0).reshape(blocks, 4, block_rows, block_rows)
    residual = anomalies.astype(jnp.float32) - jnp.einsum(
        "bjmq,bjqr->bmr", picked, gathered, preferred_element_type=jnp.float32
    )
    squares = jnp.sum(residual * residual, axis=1)
    totals = taken_together(squares, TILE)
    variances = totals / members + EPSILON
    weighted = (residual / variances[:, None, :]).astype(jnp.bfloat16)
    returned = jnp.einsum("bmr,bjqr->bjmq", weighted, gathered, preferred_element_type=jnp.float32)
    member_shape = anomalies.shape[1:]
    collected = jnp.zeros((5 * blocks,) + member_shape, jnp.float32)
    collected = collected.at[local_index.reshape(-1)].add(
        returned.reshape((4 * blocks,) + member_shape)
    )

    def portion(offset):
        return collected[(4 - offset) * blocks : (5 - offset) * blocks]

    incoming = portion(0)
    for offset in range(1, 5):
        incoming = incoming + from_behind(
            portion(offset).astype(jnp.bfloat16), "blk", -offset
        ).astype(jnp.float32)
    applied = weighted.astype(jnp.float32) - incoming
    return (applied, coefficients, variances)


def solution(mesh):
    split = Mesh(mesh.devices.reshape(mesh.shape["blk"], 4, 2), ("blk", "tile_0", "tile_1"))
    return jax.shard_map(
        local,
        mesh=split,
        in_specs=(P("blk", TILE, None), P("blk", None)),
        out_specs=(P("blk", TILE, None), P(BLK_TILE, None, None), P("blk", None)),
        check_vma=False,
    )
```

profile of v0, /device:TPU:1, one launch (start us, length us, event | category | flops | bytes accessed | tf_op | source)
XLA Modules:
  0.0 472.8 jit_solution(6829718036199443438)
XLA Ops:
  12.3 76.4 %collective-permute-done = bf16[8,256,128]{2,1,0:T(8,128)(2,1)S(1)} collective-permute-done((bf16[8,256,128]{2,1,0:T(8,128)(2,1)}, bf16[8,256,128]{2,1,0:T(8,128)(2,1)S(1)}, u32[]{:S(2)}, u32[]{:S(2)}) %collective-permute-start) | collective-permute-done | bytes 524320 | tf_op jit(solution)/shard_map/ppermute | solution.py:18
  97.2 7.0 %all_to_all.20 = bf16[4,2,1,5,256,128]{5,4,0,3,2,1:T(8,128)(2,1)S(1)} all-to-all(bf16[4,2,1,5,256,128]{5,4,0,3,2,1:T(8,128)(2,1)S(1)} %copy.87), channel_id=1, replica_groups=mesh['blk'=32,'tile_0'=4,'tile_1'=2] {'tile_1'}, dimensions={1} | all-to-all | bytes 5242880 | tf_op jit(solution)/shard_map/all_to_all | solution.py:37
  106.0 4.0 all-to-all-start.1
  110.5 30.9 %all-to-all-done.1 = bf16[4,2,1,5,256,128]{5,4,1,3,2,0:T(8,128)(2,1)S(1)} async-done(((bf16[4,2,1,5,256,128]{5,4,1,3,2,0:T(8,128)(2,1)}), bf16[4,2,1,5,256,128]{5,4,1,3,2,0:T(8,128)(2,1)S(1)}, u32[]{:S(2)}, u32[]{:S(2)}) %all-to-all-start.1) | async-done | bytes 2621472 | tf_op jit(solution)/shard_map/all_to_all | solution.py:37
  151.7 11.7 %custom-call.36 = f32[1,128,128]{2,1,0:T(8,128)S(1)} custom-call(f32[1,128,128]{2,1,0:T(8,128)S(1)} %cholesky.264), custom_call_target="Cholesky" | custom-call | tf_op jit(solution)/shard_map/jit(cholesky)/cholesky | solution.py:67
  163.5 9.8 %custom-call.37 = f32[1,1,128,128]{2,3,1,0:T(8,128)S(1)} custom-call(f32[1,1,128,128]{3,2,1,0:T(8,128)S(1)} %get-tuple-element.58), custom_call_target="InvertDiagBlocksLowerTriangular" | custom-call | tf_op jit(solution)/shard_map/jit(cholesky)/cholesky | solution.py:67
  174.2 11.9 %custom-call.38 = f32[1,128,128]{2,1,0:T(8,128)S(1)} custom-call(f32[1,128,128]{2,1,0:T(8,128)S(1)} %cholesky.268), custom_call_target="Cholesky" | custom-call | tf_op jit(solution)/shard_map/jit(cholesky)/cholesky | solution.py:67
  186.2 10.4 %custom-call.39 = f32[1,1,128,128]{2,3,1,0:T(8,128)} custom-call(f32[1,1,128,128]{3,2,1,0:T(8,128)S(1)} %get-tuple-element.56), custom_call_target="InvertDiagBlocksLowerTriangular" | custom-call | tf_op jit(solution)/shard_map/jit(cholesky)/cholesky | solution.py:67
  200.2 13.2 %custom-call.40 = f32[1,128,128]{2,1,0:T(8,128)} custom-call(f32[1,128,128]{2,1,0:T(8,128)} %cholesky.273), custom_call_target="Cholesky" | custom-call | tf_op jit(solution)/shard_map/jit(cholesky)/cholesky | solution.py:67
  217.8 11.3 %custom-call.41 = f32[1,1,128,128]{2,3,1,0:T(8,128)} custom-call(f32[1,1,128,128]{3,2,1,0:T(8,128)} %get-tuple-element.54), custom_call_target="InvertDiagBlocksLowerTriangular" | custom-call | tf_op jit(solution)/shard_map/jit(cholesky)/cholesky | solution.py:67
  230.7 12.1 %custom-call.42 = f32[1,128,128]{2,1,0:T(8,128)S(1)} custom-call(f32[1,128,128]{2,1,0:T(8,128)S(1)} %fusion.19), custom_call_target="Cholesky" | custom-call | tf_op jit(solution)/shard_map/jit(cholesky)/cholesky | solution.py:67
  248.8 11.1 %while.1 = (s32[]{:T(128)}, f32[1,512,512]{1,2,0:T(8,128)S(1)}, s32[4,2]{0,1:T(2,128)S(1)}, f32[4,1,128,128]{3,2,1,0:T(8,128)}, s32[]{:T(128)}) while((s32[]{:T(128)}, f32[1,512,512]{1,2,0:T(8,128)S(1)}, s32[4,2]{0,1:T(2,128)S(1)}, f32[4,1,128,128]{3,2,1,0:T(8,128)}, s32[]{:T(128)}) %tuple.43), condition=%wide.while_cond, body=%wide.while_body.sunk | while | flops 2 | bytes 393333 | solution.py:69
  259.9 40.1 %custom-call.43 = f32[1,4,128,128]{2,3,1,0:T(8,128)S(1)} custom-call(f32[1,4,128,128]{3,2,1,0:T(8,128)} %bitcast.239), custom_call_target="InvertDiagBlocksLowerTriangular" | custom-call | tf_op jit(solution)/shard_map/triangular_solve | solution.py:69
  307.8 5.0 %all-to-all-start.2 = ((bf16[8,1,512,128]{3,2,1,0:T(8,128)(2,1)}), bf16[8,1,512,128]{3,2,1,0:T(8,128)(2,1)S(1)}, u32[]{:S(2)}, u32[]{:S(2)}) async-start(bf16[8,1,512,128]{3,2,1,0:T(8,128)(2,1)} %broadcast_in_dim.47), calls=%async_computation.2 | async-start | bytes 2097152 | tf_op jit(solution)/shard_map/all_to_all | solution.py:49
  313.1 14.7 %all-to-all-done.2 = bf16[8,1,512,128]{3,2,1,0:T(8,128)(2,1)S(1)} async-done(((bf16[8,1,512,128]{3,2,1,0:T(8,128)(2,1)}), bf16[8,1,512,128]{3,2,1,0:T(8,128)(2,1)S(1)}, u32[]{:S(2)}, u32[]{:S(2)}) %all-to-all-start.2) | async-done | bytes 1048608 | tf_op jit(solution)/shard_map/all_to_all | solution.py:49
  331.2 4.4 all-to-all-start.3
  335.6 4.7 all-to-all-done.3
  344.2 5.4 %copy.104 = f32[8,4,256,128]{3,2,1,0:T(8,128)} copy(f32[8,4,256,128]{2,3,1,0:T(8,128)} %convolution_bitcast_fusion) | data formatting | bytes 8388608 | tf_op jit(solution)/shard_map/bmr,bjqr->bjmq/transpose | solution.py:109
  352.5 9.9 %scatter_fusion = f32[40,256,128]{2,1,0:T(8,128)} fusion(f32[40,256,128]{2,1,0:T(8,128)} %broadcast_in_dim.49, s32[32]{0:T(128)S(1)} %fusion.51, f32[32,256,128]{2,1,0:T(8,128)} %bitcast.217), kind=kCustom, calls=%fused_computation.1 | custom fusion | flops 1048576 | bytes 12583040 | tf_op jit(solution)/shard_map/scatter-add | solution.py:112
  365.6 13.6 %collective-permute-start.7 = (bf16[8,256,128]{2,1,0:T(8,128)(2,1)S(1)}, bf16[8,256,128]{2,1,0:T(8,128)(2,1)S(1)}, u32[]{:S(2)}, u32[]{:S(2)}) collective-permute-start(bf16[8,256,128]{2,1,0:T(8,128)(2,1)S(1)} %get-tuple-element.44), channel_id=1, source_target_pairs={{32,0},{40,8},{48,16},{56,24},{64,32},{72,40},{80,48},{88,56},{96,... | collective-permute-start | bytes 1572872 | tf_op jit(solution)/shard_map/ppermute | solution.py:18
  379.3 6.4 %collective-permute-start.5 = (bf16[8,256,128]{2,1,0:T(8,128)(2,1)S(1)}, bf16[8,256,128]{2,1,0:T(8,128)(2,1)S(1)}, u32[]{:S(2)}, u32[]{:S(2)}) collective-permute-start(bf16[8,256,128]{2,1,0:T(8,128)(2,1)S(1)} %get-tuple-element.46), channel_id=1, source_target_pairs={{16,0},{24,8},{32,16},{40,24},{48,32},{56,40},{64,48},{72,56},{80,... | collective-permute-start | bytes 1572872 | tf_op jit(solution)/shard_map/ppermute | solution.py:18
  386.3 14.5 %collective-permute-done.7 = bf16[8,256,128]{2,1,0:T(8,128)(2,1)S(1)} collective-permute-done((bf16[8,256,128]{2,1,0:T(8,128)(2,1)S(1)}, bf16[8,256,128]{2,1,0:T(8,128)(2,1)S(1)}, u32[]{:S(2)}, u32[]{:S(2)}) %collective-permute-start.7) | collective-permute-done | bytes 524320 | tf_op jit(solution)/shard_map/ppermute | solution.py:18
  400.8 34.5 %collective-permute-done.6 = bf16[8,256,128]{2,1,0:T(8,128)(2,1)S(1)} collective-permute-done((bf16[8,256,128]{2,1,0:T(8,128)(2,1)S(1)}, bf16[8,256,128]{2,1,0:T(8,128)(2,1)S(1)}, u32[]{:S(2)}, u32[]{:S(2)}) %collective-permute-start.6) | collective-permute-done | bytes 524320 | tf_op jit(solution)/shard_map/ppermute | solution.py:18
  435.3 34.7 %collective-permute-done.5 = bf16[8,256,128]{2,1,0:T(8,128)(2,1)S(1)} collective-permute-done((bf16[8,256,128]{2,1,0:T(8,128)(2,1)S(1)}, bf16[8,256,128]{2,1,0:T(8,128)(2,1)S(1)}, u32[]{:S(2)}, u32[]{:S(2)}) %collective-permute-start.5) | collective-permute-done | bytes 524320 | tf_op jit(solution)/shard_map/ppermute | solution.py:18
  (134 shorter events, 82.3 us)
Async XLA Ops:
  0.6 91.4 %copy-start.4 = (bf16[8,256,128]{2,1,0:T(8,128)(2,1)S(1)}, bf16[8,256,128]{2,1,0:T(8,128)(2,1)}, u32[]{:S(2)}) copy-start(bf16[8,256,128]{2,1,0:T(8,128)(2,1)} %param.2) | copy-start | bytes 1572868
  0.6 90.5 %collective-permute-start.3 = (bf16[8,256,128]{2,1,0:T(8,128)(2,1)}, bf16[8,256,128]{2,1,0:T(8,128)(2,1)S(1)}, u32[]{:S(2)}, u32[]{:S(2)}) collective-permute-start(bf16[8,256,128]{2,1,0:T(8,128)(2,1)} %param.2), channel_id=1, source_target_pairs={{248,0},{0,8},{8,16},{16,24},{24,32},{32,40},{40,48},{48,56},{56,6... | collective-permute-start | bytes 1572872 | tf_op jit(solution)/shard_map/ppermute | solution.py:18
  3.2 87.2 %collective-permute-start.2 = (bf16[8,256,128]{2,1,0:T(8,128)(2,1)}, bf16[8,256,128]{2,1,0:T(8,128)(2,1)S(1)}, u32[]{:S(2)}, u32[]{:S(2)}) collective-permute-start(bf16[8,256,128]{2,1,0:T(8,128)(2,1)} %param.2), channel_id=1, source_target_pairs={{240,0},{248,8},{0,16},{8,24},{16,32},{24,40},{32,48},{40,56},{48,... | collective-permute-start | bytes 1572872 | tf_op jit(solution)/shard_map/ppermute | solution.py:18
  6.2 83.3 %collective-permute-start.1 = (bf16[8,256,128]{2,1,0:T(8,128)(2,1)}, bf16[8,256,128]{2,1,0:T(8,128)(2,1)S(1)}, u32[]{:S(2)}, u32[]{:S(2)}) collective-permute-start(bf16[8,256,128]{2,1,0:T(8,128)(2,1)} %param.2), channel_id=1, source_target_pairs={{232,0},{240,8},{248,16},{0,24},{8,32},{16,40},{24,48},{32,56},{40... | collective-permute-start | bytes 1572872 | tf_op jit(solution)/shard_map/ppermute | solution.py:18
  9.9 78.7 %collective-permute-start = (bf16[8,256,128]{2,1,0:T(8,128)(2,1)}, bf16[8,256,128]{2,1,0:T(8,128)(2,1)S(1)}, u32[]{:S(2)}, u32[]{:S(2)}) collective-permute-start(bf16[8,256,128]{2,1,0:T(8,128)(2,1)} %param.2), channel_id=1, source_target_pairs={{224,0},{232,8},{240,16},{248,24},{0,32},{8,40},{16,48},{24,56},{3... | collective-permute-start | bytes 1572872 | tf_op jit(solution)/shard_map/ppermute | solution.py:18
  95.5 1.3 copy-start.1
  106.0 35.4 %all-to-all-start.1 = ((bf16[4,2,1,5,256,128]{5,4,1,3,2,0:T(8,128)(2,1)}), bf16[4,2,1,5,256,128]{5,4,1,3,2,0:T(8,128)(2,1)S(1)}, u32[]{:S(2)}, u32[]{:S(2)}) async-start(bf16[4,2,1,5,256,128]{5,4,1,3,2,0:T(8,128)(2,1)} %copy.88), calls=%async_computation.1 | async-start | bytes 5242880 | tf_op jit(solution)/shard_map/all_to_all | solution.py:37
  141.6 1.5 copy-start
  173.8 12.4 %copy-start.5 = (f32[384,128]{0,1:T(8,128)}, f32[384,128]{0,1:T(8,128)S(1)}, u32[]{:S(2)}) copy-start(f32[384,128]{0,1:T(8,128)S(1)} %copy.92) | copy-start | bytes 589828
  174.1 12.1 %copy-start.7 = (f32[1,384,128]{2,1,0:T(8,128)}, f32[1,384,128]{2,1,0:T(8,128)S(1)}, u32[]{:S(2)}) copy-start(f32[1,384,128]{2,1,0:T(8,128)S(1)} %fusion.9) | copy-start | bytes 589828
  300.0 2.6 copy-start.6
  302.8 25.0 %copy-start.2 = (bf16[32,256,128]{2,1,0:T(8,128)(2,1)S(1)}, bf16[32,256,128]{2,1,0:T(8,128)(2,1)}, u32[]{:S(2)}) copy-start(bf16[32,256,128]{2,1,0:T(8,128)(2,1)} %copy-done.1) | copy-start | bytes 6291460
  307.8 20.0 %all-to-all-start.2 = ((bf16[8,1,512,128]{3,2,1,0:T(8,128)(2,1)}), bf16[8,1,512,128]{3,2,1,0:T(8,128)(2,1)S(1)}, u32[]{:S(2)}, u32[]{:S(2)}) async-start(bf16[8,1,512,128]{3,2,1,0:T(8,128)(2,1)} %broadcast_in_dim.47), calls=%async_computation.2 | async-start | bytes 2097152 | tf_op jit(solution)/shard_map/all_to_all | solution.py:49
  331.2 9.1 %all-to-all-start.3 = ((f32[8,8,128]{2,1,0:T(8,128)}), f32[8,8,128]{2,1,0:T(8,128)S(1)}, u32[]{:S(2)}, u32[]{:S(2)}) async-start(f32[8,8,128]{2,1,0:T(8,128)} %broadcast_in_dim.48), calls=%async_computation.3 | async-start | bytes 65536 | tf_op jit(solution)/shard_map/all_to_all | solution.py:49
  340.3 129.6 %copy-start.8 = (f32[8,128]{1,0:T(8,128)}, f32[8,128]{1,0:T(8,128)S(1)}, u32[]{:S(2)}) copy-start(f32[8,128]{1,0:T(8,128)S(1)} %multiply_add_fusion) | copy-start | bytes 12292
  365.4 104.6 %copy-start.3 = (f32[8,256,128]{2,1,0:T(8,128)S(1)}, f32[8,256,128]{2,1,0:T(8,128)}, u32[]{:S(2)}) copy-start(f32[8,256,128]{2,1,0:T(8,128)} %get-tuple-element.63) | copy-start | bytes 3145732
  365.6 20.8 %collective-permute-start.4 = (bf16[8,256,128]{2,1,0:T(8,128)(2,1)S(1)}, bf16[8,256,128]{2,1,0:T(8,128)(2,1)S(1)}, u32[]{:S(2)}, u32[]{:S(2)}) collective-permute-start(bf16[8,256,128]{2,1,0:T(8,128)(2,1)S(1)} %get-tuple-element.43), channel_id=1, source_target_pairs={{8,0},{16,8},{24,16},{32,24},{40,32},{48,40},{56,48},{64,56},{72,6... | collective-permute-start | bytes 1572872 | tf_op jit(solution)/shard_map/ppermute | solution.py:18
  365.6 35.1 %collective-permute-start.7 = (bf16[8,256,128]{2,1,0:T(8,128)(2,1)S(1)}, bf16[8,256,128]{2,1,0:T(8,128)(2,1)S(1)}, u32[]{:S(2)}, u32[]{:S(2)}) collective-permute-start(bf16[8,256,128]{2,1,0:T(8,128)(2,1)S(1)} %get-tuple-element.44), channel_id=1, source_target_pairs={{32,0},{40,8},{48,16},{56,24},{64,32},{72,40},{80,48},{88,56},{96,... | collective-permute-start | bytes 1572872 | tf_op jit(solution)/shard_map/ppermute | solution.py:18
  379.3 56.0 %collective-permute-start.6 = (bf16[8,256,128]{2,1,0:T(8,128)(2,1)S(1)}, bf16[8,256,128]{2,1,0:T(8,128)(2,1)S(1)}, u32[]{:S(2)}, u32[]{:S(2)}) collective-permute-start(bf16[8,256,128]{2,1,0:T(8,128)(2,1)S(1)} %get-tuple-element.45), channel_id=1, source_target_pairs={{24,0},{32,8},{40,16},{48,24},{56,32},{64,40},{72,48},{80,56},{88,... | collective-permute-start | bytes 1572872 | tf_op jit(solution)/shard_map/ppermute | solution.py:18
  379.3 90.7 %collective-permute-start.5 = (bf16[8,256,128]{2,1,0:T(8,128)(2,1)S(1)}, bf16[8,256,128]{2,1,0:T(8,128)(2,1)S(1)}, u32[]{:S(2)}, u32[]{:S(2)}) collective-permute-start(bf16[8,256,128]{2,1,0:T(8,128)(2,1)S(1)} %get-tuple-element.46), channel_id=1, source_target_pairs={{16,0},{24,8},{32,16},{40,24},{48,32},{56,40},{64,48},{72,56},{80,... | collective-permute-start | bytes 1572872 | tf_op jit(solution)/shard_map/ppermute | solution.py:18
where the time goes:
time: 479 us; the launch traced here: 473 us
  waiting for transfers between devices  210 us (44%)
  other arithmetic  144 us (30%)
  starting transfers between devices  44 us (9%)
  local copies, waits for them, and re-layouts  43.4 us (9%)
  matrix products  20.4 us (4%)
  blocking collectives  7.02 us (1%)
    ppermute x8, waiting for transfers between devices, from_behind(): return lax.ppermute(block, axis, route)  160 us
    another operation x14, other arithmetic, solve_blocks(): factor = jnp.linalg.cholesky(gram_part)  85.2 us
    another operation x5, other arithmetic, solve_blocks(): lax.linalg.triangular_solve(factor, middle, left_side=True, lower=True, t...  41.5 us
    all_to_all x1, waiting for transfers between devices, moved_by_axis(): lax.all_to_all(tiles, axes[k], split_axis=k, concat_axis=k, tiled=True)  30.9 us
    ppermute x8, starting transfers between devices, from_behind(): return lax.ppermute(block, axis, route)  30.6 us
    all_to_all x2, waiting for transfers between devices, copy_for_each(): lax.all_to_all(jnp.broadcast_to(value[None], (peers, *value.shape)), axis...  19.4 us
    another operation x20, local copies, waits for them, and re-layouts  11 us
    scatter-add x1, other arithmetic, local(): collected.at[local_index.reshape(-1)]  9.94 us
  transfers between devices with their start and end apart: 11, of which 7 were waited for; matrix products, arithmetic and copies ran while one was open for 1% of the time, Pallas kernels for 0%

commit v1 on v0

v1 whole, which is shorter than its diff:
```python
import jax
import jax.numpy as jnp
from jax import lax
from jax.experimental import pallas as pl
from jax.experimental.pallas import tpu as pltpu
from jax.sharding import Mesh
from jax.sharding import PartitionSpec as P

TILE = ("tile_0", "tile_1")
BLK_TILE = ("blk", "tile_0", "tile_1")
MESH = pl.DeviceIdType.MESH

RIDGE_TERM = 0.25
EPSILON = 1e-05
HI = lax.Precision.HIGHEST
R = 128
SLOTS = 4
REACH = 4
CHUNKS = 8
VM = pl.BlockSpec(memory_space=pltpu.VMEM)
SM = pl.BlockSpec(memory_space=pltpu.SMEM)


def remote(src, dst, send_sem, recv_sem, where):
    return pltpu.make_async_remote_copy(
        src_ref=src, dst_ref=dst, send_sem=send_sem, recv_sem=recv_sem, device_id=where, device_id_type=MESH
    )


def places():
    n, cores = lax.axis_size("blk"), lax.axis_size("tile_1")
    peers = lax.axis_size("tile_0") * cores
    return lax.axis_index("blk"), n, lax.axis_index("tile_0") * cores + lax.axis_index("tile_1"), peers, cores


def tile_place(t, cores):
    return {"tile_0": lax.div(t, cores), "tile_1": lax.rem(t, cores)}


def meet(targets):
    barrier = pltpu.get_barrier_semaphore()
    for where in targets:
        pl.semaphore_signal(barrier, inc=1, device_id=where, device_id_type=MESH)
    pl.semaphore_wait(barrier, len(targets))


def spread_kernel(index_ref, a_ref, picked_ref, solve_ref, *rest):
    windows = rest[:CHUNKS]
    ring_send, ring_recv, out_send, out_recv = rest[CHUNKS:]
    p, n, t, peers, cores = places()
    blocks, members = a_ref.shape[0], a_ref.shape[1]
    rows = members // CHUNKS
    following, previous = lax.rem(p + 1, n), lax.rem(p + n - 1, n)
    others = [lax.rem(t + e, peers) for e in range(1, peers)]
    meet([{"blk": following}, {"blk": previous}] + [tile_place(o, cores) for o in others])

    def hop(c, r):
        low, high = (REACH - r) * blocks, (REACH + 1 - r) * blocks
        if r == 1:
            source = a_ref.at[:, c * rows : (c + 1) * rows, :]
        else:
            source = windows[c].at[low + blocks : high + blocks]
        return remote(
            source, windows[c].at[low:high], ring_send.at[c, r - 1], ring_recv.at[c, r - 1], {"blk": following}
        )

    def give(c, e):
        to = others[e - 1]
        span = pl.ds(c * rows, rows)
        return remote(
            picked_ref.at[to, span], solve_ref.at[t, span], out_send.at[c, e - 1], out_recv.at[c, e - 1],
            tile_place(to, cores),
        )

    def pick(c):
        span = slice(c * rows, (c + 1) * rows)
        for k in range(blocks):
            for j in range(SLOTS):
                picked_ref[k, span, j * R : (j + 1) * R] = windows[c][index_ref[k, j]]
            picked_ref[k, span, SLOTS * R :] = a_ref[k, span, :]

    for c in range(CHUNKS):
        windows[c][REACH * blocks :] = a_ref[:, c * rows : (c + 1) * rows, :]
    for step in range(CHUNKS + REACH):
        for r in range(1, REACH + 1):
            c = step - (r - 1)
            if 0 <= c < CHUNKS:
                if r > 1:
                    hop(c, r - 1).wait_recv()
                hop(c, r).start()
        c = step - REACH
        if 0 <= c < CHUNKS:
            hop(c, REACH).wait_recv()
            pick(c)
            for e in range(1, peers):
                give(c, e).start()
    solve_ref[t] = picked_ref[t]
    for c in range(CHUNKS):
        for e in range(1, peers):
            give(c, e).wait_recv()
    for c in range(CHUNKS):
        for r in range(1, REACH + 1):
            hop(c, r).wait_send()
        for e in range(1, peers):
            give(c, e).wait_send()


def spread(index, anomalies, peers):
    blocks, members, _ = anomalies.shape
    width = (SLOTS + 1) * R
    dma = pltpu.SemaphoreType.DMA
    return pl.pallas_call(
        spread_kernel,
        out_shape=(
            jax.ShapeDtypeStruct((blocks, members, width), jnp.bfloat16),
            jax.ShapeDtypeStruct((peers, members, width), jnp.bfloat16),
        ),
        in_specs=[SM, VM],
        out_specs=(VM, VM),
        scratch_shapes=[
            pltpu.VMEM(((REACH + 1) * blocks, members // CHUNKS, R), jnp.bfloat16) for _ in range(CHUNKS)
        ]
        + [dma((CHUNKS, REACH)), dma((CHUNKS, REACH)), dma((CHUNKS, peers - 1)), dma((CHUNKS, peers - 1))],
        compiler_params=pltpu.CompilerParams(collective_id=0, has_side_effects=True),
        name="spread",
    )(index, anomalies)


def invert_block(d):
    sub = lax.broadcasted_iota(jnp.int32, (8, 128), 0)
    lane = lax.broadcasted_iota(jnp.int32, (8, 128), 1)
    groups = d.shape[0] // 8
    rows = [d[8 * g : 8 * g + 8, :] for g in range(groups)]

    def across(v, c):
        return jnp.broadcast_to(v[:, c : c + 1], (8, 128))

    def down(v, s):
        return jnp.broadcast_to(v[s : s + 1, :], (8, 128))

    for q in range(groups):
        p = rows[q]
        t = [across(p, 8 * q + c) for c in range(8)]
        for s in range(8):
            inv = 1.0 / down(t[s], s)
            at = lane == 8 * q + s
            row = jnp.where(at, inv, down(p, s) * inv)
            p = jnp.where(sub == s, row, jnp.where(at, 0.0, p) - t[s] * row)
            for c in range(s + 1, 8):
                n = down(t[c], s) * inv
                t[c] = jnp.where(sub == s, n, t[c] - t[s] * n)
        b = [down(p, s) for s in range(8)]
        panel = (lane >= 8 * q) & (lane < 8 * q + 8)
        for g in range(groups):
            if g == q:
                continue
            old = rows[g]
            new = jnp.where(panel, 0.0, old)
            for s in range(8):
                new = new - across(old, 8 * q + s) * b[s]
            rows[g] = new
        rows[q] = p
    return jnp.concatenate(rows, axis=0)


def mm(a, b, dims=((1,), (0,))):
    return lax.dot_general(a, b, (dims, ((), ())), precision=HI, preferred_element_type=jnp.float32)


def solve_kernel(x_ref, coef_ref, var_ref, s_ref, w_ref):
    members = x_ref.shape[0]
    x = x_ref[...]
    g = lax.dot_general(x[:, : 4 * R], x, (((0,), (0,)), ((), ())), preferred_element_type=jnp.float32)
    s_ref[...] = g * (1.0 / members)
    eye = lax.broadcasted_iota(jnp.int32, (R, R), 0) == lax.broadcasted_iota(jnp.int32, (R, R), 1)
    ridge = jnp.where(eye, RIDGE_TERM, 0.0)

    def step(i, carry):
        lo = pl.multiple_of(i * R, R)
        w_ref[i] = invert_block(s_ref[pl.ds(lo, R), pl.ds(lo, R)] + ridge)
        for c in range(4):
            @pl.when(i == c)
            def _(c=c):
                a, z = c * R, (c + 1) * R
                w = w_ref[c]
                u = mm(w, s_ref[a:z, z:])
                if c < 3:
                    s_ref[z:, z:] -= mm(s_ref[a:z, z : 4 * R], u, ((0,), (0,)))
                s_ref[a:z, z:] = u
        return carry

    lax.fori_loop(0, 4, step, 0)
    for c in range(2, -1, -1):
        a, z = c * R, (c + 1) * R
        s_ref[a:z, 4 * R :] -= mm(s_ref[a:z, z : 4 * R], s_ref[z : 4 * R, 4 * R :])
    coef = s_ref[:, 4 * R :].astype(jnp.bfloat16)
    coef_ref[...] = coef
    resid = x[:, 4 * R :].astype(jnp.float32) - jnp.dot(x[:, : 4 * R], coef, preferred_element_type=jnp.float32)
    total = jnp.sum(resid * resid, axis=0, keepdims=True)
    var_ref[...] = jnp.broadcast_to(total * (1.0 / members) + EPSILON, var_ref.shape)


def solve(x):
    members, width = x.shape
    return pl.pallas_call(
        solve_kernel,
        out_shape=(jax.ShapeDtypeStruct((512, 128), jnp.bfloat16), jax.ShapeDtypeStruct((8, 128), jnp.float32)),
        in_specs=[VM],
        out_specs=(VM, VM),
        scratch_shapes=[pltpu.VMEM((512, 640), jnp.float32), pltpu.VMEM((4, 128, 128), jnp.float32)],
        name="solve",
    )(x)


def gather_kernel(coef_ref, var_ref, all_ref, vars_ref, send, recv, var_send, var_recv):
    p, n, t, peers, cores = places()
    chips = peers // cores
    x, core = lax.axis_index("tile_0"), lax.axis_index("tile_1")
    right, left = lax.rem(x + 1, chips), lax.rem(x + chips - 1, chips)
    other = 1 - core
    others = [lax.rem(t + e, peers) for e in range(1, peers)]
    meet([tile_place(o, cores) for o in others])
    half = coef_ref.shape[0] // 2
    far = lax.rem(x + 2, chips)

    def place(chip):
        return chip * cores + core

    def variance(e):
        return remote(var_ref, vars_ref.at[t], var_send.at[e - 1], var_recv.at[e - 1], tile_place(others[e - 1], cores))

    low, high = slice(0, half), slice(half, 2 * half)
    to_right = [
        remote(coef_ref.at[part], all_ref.at[t, part], send.at[i], recv.at[i], {"tile_0": right})
        for i, part in ((0, low), (1, high))
    ]
    to_left = [
        remote(coef_ref.at[part], all_ref.at[t, part], send.at[i], recv.at[i], {"tile_0": left})
        for i, part in ((2, high), (3, low))
    ]
    on_right = remote(
        all_ref.at[place(left), low], all_ref.at[place(left), low], send.at[4], recv.at[4], {"tile_0": right}
    )
    on_left = remote(
        all_ref.at[place(right), high], all_ref.at[place(right), high], send.at[5], recv.at[5], {"tile_0": left}
    )

    def across(i, chip, part):
        view = all_ref.at[place(chip), part]
        return remote(view, view, send.at[i], recv.at[i], {"tile_1": other})

    own = remote(coef_ref, all_ref.at[t], send.at[6], recv.at[6], {"tile_1": other})
    to_right[0].start()
    to_left[0].start()
    to_right[1].start()
    to_left[1].start()
    own.start()
    for e in range(1, peers):
        variance(e).start()
    all_ref[t] = coef_ref[...]
    vars_ref[t] = var_ref[...]
    steps = [
        (to_right[0], on_right, across(7, left, low)),
        (to_left[0], on_left, across(8, right, high)),
        (to_right[1], None, across(9, left, high)),
        (to_left[1], None, across(10, right, low)),
        (on_right, None, across(11, far, low)),
        (on_left, None, across(12, far, high)),
    ]
    for arrived, forward, sideways in steps:
        arrived.wait_recv()
        if forward is not None:
            forward.start()
        sideways.start()
    for _, _, sideways in steps:
        sideways.wait_recv()
    own.wait_recv()
    for e in range(1, peers):
        variance(e).wait_recv()
    for arrived, _, sideways in steps:
        arrived.wait_send()
        sideways.wait_send()
    own.wait_send()
    for e in range(1, peers):
        variance(e).wait_send()


def gather(coef, var, peers):
    dma = pltpu.SemaphoreType.DMA
    return pl.pallas_call(
        gather_kernel,
        out_shape=(
            jax.ShapeDtypeStruct((peers,) + coef.shape, coef.dtype),
            jax.ShapeDtypeStruct((peers,) + var.shape, var.dtype),
        ),
        in_specs=[VM, VM],
        out_specs=(VM, VM),
        scratch_shapes=[dma((13,)), dma((13,)), dma((peers - 1,)), dma((peers - 1,))],
        compiler_params=pltpu.CompilerParams(collective_id=1, has_side_effects=True),
        name="gather",
    )(coef, var)


def weigh_kernel(index_ref, picked_ref, coef_ref, var_ref, own_ref, near_ref, far_ref, sums_ref):
    blocks = picked_ref.shape[0]
    sums_ref[...] = jnp.zeros_like(sums_ref)

    def block(k, carry):
        coef = coef_ref[k]
        resid = picked_ref[k, :, SLOTS * R :].astype(jnp.float32) - jnp.dot(
            picked_ref[k, :, : SLOTS * R], coef, preferred_element_type=jnp.float32
        )
        weighted = (resid / var_ref[k, 0:1, :]).astype(jnp.bfloat16)
        own_ref[k] = weighted.astype(jnp.float32)
        terms = lax.dot_general(weighted, coef, (((1,), (1,)), ((), ())), preferred_element_type=jnp.float32)
        for j in range(SLOTS):
            sums_ref[index_ref[k, j]] += terms[:, j * R : (j + 1) * R]
        return carry

    lax.fori_loop(0, blocks, block, 0)
    far_ref[...] = sums_ref[:blocks].astype(jnp.bfloat16)
    near_ref[...] = sums_ref[blocks : REACH * blocks]
    own_ref[...] -= sums_ref[REACH * blocks :]


def weigh(index, picked, coef, var):
    blocks, members, _ = picked.shape
    f32 = jnp.float32
    return pl.pallas_call(
        weigh_kernel,
        out_shape=(
            jax.ShapeDtypeStruct((blocks, members, R), f32),
            jax.ShapeDtypeStruct(((REACH - 1) * blocks, members, R), f32),
            jax.ShapeDtypeStruct((blocks, members, R), jnp.bfloat16),
        ),
        in_specs=[SM, VM, VM, VM],
        out_specs=(VM, VM, VM),
        scratch_shapes=[pltpu.VMEM(((REACH + 1) * blocks, members, R), f32)],
        name="weigh",
    )(index, picked, coef, var)


def collect_kernel(near_ref, far_ref, sum_ref, staged, landed, send, recv):
    p, n, t, peers, cores = places()
    following, previous = lax.rem(p + 1, n), lax.rem(p + n - 1, n)
    meet([{"blk": following}, {"blk": previous}])
    blocks, members, _ = far_ref.shape
    rows = members // CHUNKS

    def hop(c, r):
        span = pl.ds(c * rows, rows)
        source = far_ref.at[:, span] if r == 1 else staged.at[r - 2, :, span]
        target = sum_ref.at[:, span] if r == REACH else landed.at[r - 1, :, span]
        return remote(source, target, send.at[c, r - 1], recv.at[c, r - 1], {"blk": previous})

    for step in range(CHUNKS + REACH - 1):
        for r in range(1, REACH + 1):
            c = step - (r - 1)
            if 0 <= c < CHUNKS:
                if r > 1:
                    hop(c, r - 1).wait_recv()
                    span = slice(c * rows, (c + 1) * rows)
                    here = near_ref[(r - 2) * blocks : (r - 1) * blocks, span]
                    staged[r - 2, :, span] = (landed[r - 2, :, span].astype(jnp.float32) + here).astype(jnp.bfloat16)
                hop(c, r).start()
    for c in range(CHUNKS):
        hop(c, REACH).wait_recv()
    for c in range(CHUNKS):
        for r in range(1, REACH + 1):
            hop(c, r).wait_send()


def collect(near, far):
    dma = pltpu.SemaphoreType.DMA
    stage = pltpu.VMEM((REACH - 1,) + far.shape, far.dtype)
    return pl.pallas_call(
        collect_kernel,
        out_shape=jax.ShapeDtypeStruct(far.shape, far.dtype),
        in_specs=[VM, VM],
        out_specs=VM,
        scratch_shapes=[stage, stage, dma((CHUNKS, REACH)), dma((CHUNKS, REACH))],
        compiler_params=pltpu.CompilerParams(collective_id=2, has_side_effects=True),
        name="collect",
    )(near, far)


def local(anomalies, predecessors):
    blocks, members, _ = anomalies.shape
    peers = lax.axis_size(TILE)
    total_blocks = blocks * lax.axis_size("blk")
    window_start = (lax.axis_index("blk") - REACH) * blocks
    index = jnp.mod(predecessors - window_start, total_blocks)
    picked, mine = spread(index, anomalies, peers)
    coef, var = solve(mine.reshape(peers * members, (SLOTS + 1) * R))
    coefs, variances = gather(coef, var, peers)
    own, near, far = weigh(index, picked, coefs, variances)
    applied = own - collect(near, far).astype(jnp.float32)
    return applied, coef[None], variances[:, 0]


def solution(mesh):
    chips = mesh.shape["tile"] // 2
    split = Mesh(mesh.devices.reshape(mesh.shape["blk"], chips, 2), ("blk", "tile_0", "tile_1"))
    return jax.shard_map(
        local,
        mesh=split,
        in_specs=(P("blk", TILE, None), P("blk", None)),
        out_specs=(P("blk", TILE, None), P(BLK_TILE, None, None), P("blk", None)),
        check_vma=False,
    )
```

time: 479 us -> 174 us (0.36); the launches traced: 473 us -> 173 us
  waiting for transfers between devices: 210 us -> 0 us
  Pallas kernels: 0 us -> 168 us
  other arithmetic: 144 us -> 2.71 us
  starting transfers between devices: 44 us -> 0 us
  local copies, waits for them, and re-layouts: 43.4 us -> 2.11 us
  matrix products: 20.4 us -> 0 us
  blocking collectives: 7.02 us -> 0 us
    pallas_call x0 -> x5, Pallas kernels: none -> 168 us  [the longest x1 71.7 us: spread(): pl.pallas_call(spread_kernel, out_shape=(jax.ShapeDtypeStruct((blocks, me...]
    ppermute x8 -> x0, waiting for transfers between devices: 160 us -> none  [from_behind(): return lax.ppermute(block, axis, route)]
    another operation x20 -> x0, other arithmetic: 130 us -> none  [the longest x14 85.2 us: solve_blocks(): factor = jnp.linalg.cholesky(gram_part)]
    all_to_all x3 -> x0, waiting for transfers between devices: 50.3 us -> none  [the longest x1 30.9 us: moved_by_axis(): lax.all_to_all(tiles, axes[k], split_axis=k, concat_axis=k, tiled=True)]
    ppermute x8 -> x0, starting transfers between devices: 30.6 us -> none  [from_behind(): return lax.ppermute(block, axis, route)]
    another operation x34 -> x0, local copies, waits for them, and re-layouts: 16.2 us -> none
    all_to_all x3 -> x0, starting transfers between devices: 13.4 us -> none  [the longest x2 9.39 us: copy_for_each(): lax.all_to_all(jnp.broadcast_to(value[None], (peers, *value.shape)), axis...]
    another operation x20 -> x0, matrix products: 10.6 us -> none  [the longest x7 4.28 us: solve_blocks(): lax.linalg.triangular_solve(factor, middle, left_side=True, lower=True, t...]
  transfers between devices with their start and end apart: 11 -> 0, of which waited for: 7 -> 0; matrix products, arithmetic and copies ran while one was open for 1% -> 0% of each run, Pallas kernels for 0% -> 0%
where the time goes in v1:
time: 174 us; the launch traced here: 173 us
  Pallas kernels  168 us (97%)
  other arithmetic  2.71 us (2%)
  local copies, waits for them, and re-layouts  2.11 us (1%)
    pallas_call x1, Pallas kernels, spread(): pl.pallas_call(spread_kernel, out_shape=(jax.ShapeDtypeStruct((blocks, me...  71.7 us
    pallas_call x1, Pallas kernels, collect(): pl.pallas_call(collect_kernel, out_shape=jax.ShapeDtypeStruct(far.shape,...  50.1 us
    pallas_call x1, Pallas kernels, solve(): pl.pallas_call(solve_kernel, out_shape=(jax.ShapeDtypeStruct((512, 128),...  25.4 us
    pallas_call x1, Pallas kernels, gather(): pl.pallas_call(gather_kernel, out_shape=(jax.ShapeDtypeStruct((peers,) +...  12.9 us
    pallas_call x1, Pallas kernels, weigh(): pl.pallas_call(weigh_kernel, out_shape=(jax.ShapeDtypeStruct((blocks, mem...  7.83 us

profile of v1, /device:TPU:1, one launch (start us, length us, event | category | flops | bytes accessed | tf_op | source)
XLA Modules:
  0.0 173.4 jit_solution(4511831644947034337)
XLA Ops:
  0.6 0.8 copy.5
  1.4 0.6 add_select_fusion.index_ref
  2.0 71.7 %spread.1 = (bf16[8,256,640]{2,1,0:T(8,128)(2,1)}, bf16[8,256,640]{2,1,0:T(8,128)(2,1)}) custom-call(s32[8,4]{1,0:T(8,128)} %add_select_fusion.index_ref, bf16[8,256,128]{2,1,0:T(8,128)(2,1)} %a_ref.1), custom_call_target="tpu_custom_call" | custom-call | tf_op jit(solution)/shard_map/spread/pallas_call | solution.py:112
  73.7 25.4 %solve.1 = (bf16[512,128]{1,0:T(8,128)(2,1)}, f32[8,128]{1,0:T(8,128)}) custom-call(bf16[2048,640]{1,0:T(8,128)(2,1)} %bitcast.3), custom_call_target="tpu_custom_call" | custom-call | tf_op jit(solution)/shard_map/solve/pallas_call | solution.py:205
  99.0 12.9 %gather.1 = (bf16[8,512,128]{2,1,0:T(8,128)(2,1)}, f32[8,8,128]{2,1,0:T(8,128)}) custom-call(bf16[512,128]{1,0:T(8,128)(2,1)} %get-tuple-element.14.coef_ref, f32[8,128]{1,0:T(8,128)} %get-tuple-element.15.var_ref), custom_call_target="tpu_custom_call" | custom-call | tf_op jit(solution)/shard_map/gather/pallas_call | solution.py:290
  111.9 7.8 %weigh.1 = (f32[8,256,128]{2,1,0:T(8,128)}, f32[24,256,128]{2,1,0:T(8,128)}, bf16[8,256,128]{2,1,0:T(8,128)(2,1)}) custom-call(s32[8,4]{1,0:T(8,128)} %add_select_fusion.index_ref, bf16[8,256,640]{2,1,0:T(8,128)(2,1)} %get-tuple-element.12.picked_ref, bf16[8,512,128]{2,1,0:T(8,128)(2,1)} %get-tuple-element.16.coef_ref, f32[8,8,128]{2,1,0:T(8,128)} %get-tuple-element.17.var_ref), custom_call_target="tpu_custom_call" | custom-call | tf_op jit(solution)/shard_map/weigh/pallas_call | solution.py:329
  119.8 0.0 copy-start
  119.8 50.1 %collect.1 = bf16[8,256,128]{2,1,0:T(8,128)(2,1)} custom-call(f32[24,256,128]{2,1,0:T(8,128)} %get-tuple-element.19.near_ref, bf16[8,256,128]{2,1,0:T(8,128)(2,1)} %get-tuple-element.20.far_ref), custom_call_target="tpu_custom_call" | custom-call | tf_op jit(solution)/shard_map/collect/pallas_call | solution.py:376
  169.9 0.0 copy-done
  169.9 2.1 %convert_subtract_fusion = f32[8,256,128]{2,1,0:T(8,128)} fusion(f32[8,256,128]{2,1,0:T(8,128)S(1)} %copy-done, bf16[8,256,128]{2,1,0:T(8,128)(2,1)} %collect.1), kind=kLoop, calls=%fused_computation | loop fusion | flops 524288 | bytes 2621440 | tf_op jit(solution)/shard_map/sub | solution.py:397
  172.0 1.4 slice.3
Async XLA Ops:
  119.8 50.2 %copy-start = (f32[8,256,128]{2,1,0:T(8,128)S(1)}, f32[8,256,128]{2,1,0:T(8,128)}, u32[]{:S(2)}) copy-start(f32[8,256,128]{2,1,0:T(8,128)} %get-tuple-element.18) | copy-start | bytes 3145732

commit v2 on v1

v2 whole, which is shorter than its diff:
```python
import jax
import jax.numpy as jnp
from jax import lax
from jax.experimental import pallas as pl
from jax.experimental.pallas import tpu as pltpu
from jax.sharding import Mesh
from jax.sharding import PartitionSpec as P

TILE = ("tile_0", "tile_1")
BLK_TILE = ("blk", "tile_0", "tile_1")
MESH = pl.DeviceIdType.MESH

RIDGE_TERM = 0.25
EPSILON = 1e-05
HI = lax.Precision.HIGHEST
R = 128
SLOTS = 4
REACH = 4
ROW = 8
VM = pl.BlockSpec(memory_space=pltpu.VMEM)
SM = pl.BlockSpec(memory_space=pltpu.SMEM)
dma = pltpu.SemaphoreType.DMA

SPREAD_SHORT, SPREAD_LONG = 11, 5
COLLECT_SHORT, COLLECT_LONG = 5, 3


def remote(src, dst, send_sem, recv_sem, where):
    return pltpu.make_async_remote_copy(
        src_ref=src, dst_ref=dst, send_sem=send_sem, recv_sem=recv_sem, device_id=where, device_id_type=MESH
    )


def places():
    n, cores = lax.axis_size("blk"), lax.axis_size("tile_1")
    peers = lax.axis_size("tile_0") * cores
    return lax.axis_index("blk"), n, lax.axis_index("tile_0") * cores + lax.axis_index("tile_1"), peers, cores


def tile_place(t, cores):
    return {"tile_0": lax.div(t, cores), "tile_1": lax.rem(t, cores)}


def meet(targets):
    barrier = pltpu.get_barrier_semaphore()
    for where in targets:
        pl.semaphore_signal(barrier, inc=1, device_id=where, device_id_type=MESH)
    pl.semaphore_wait(barrier, len(targets))


def order(short, long, short_step, short_hop, long_step, long_hop, closing):
    plan = []
    for is_long, chunks, hops, step, hop in (
        (False, short, REACH, short_step, short_hop),
        (True, long, ROW, long_step, long_hop),
    ):
        for c in range(chunks):
            for r in range(1, hops + 1 + closing):
                plan.append((step * c + hop * (r - 1), is_long, c, r))
    return [entry[1:] for entry in sorted(plan)]


def spread_kernel(pred_ref, a_ref, picked_ref, theirs_ref, own_ref, *rest):
    chunks = SPREAD_SHORT + SPREAD_LONG
    windows = rest[:chunks]
    relays = rest[chunks : chunks + SPREAD_LONG]
    short_send, short_recv, long_send, long_recv, out_send, out_recv, own_send, own_recv = rest[chunks + SPREAD_LONG :]
    p, n, t, peers, cores = places()
    blocks, members = a_ref.shape[0], a_ref.shape[1]
    rows = members // chunks
    following, previous = lax.rem(p + 1, n), lax.rem(p + n - 1, n)
    beyond, behind = lax.rem(p + ROW, n), lax.rem(p + n - ROW, n)
    others = [lax.rem(t + e, peers) for e in range(1, peers)]
    meet([{"blk": b} for b in (following, previous, beyond, behind)] + [tile_place(o, cores) for o in others])

    def part(distance):
        return slice((REACH - distance) * blocks, (REACH + 1 - distance) * blocks)

    def span(u):
        return slice(u * rows, (u + 1) * rows)

    def short_hop(c, r):
        source = a_ref.at[:, span(c)] if r == 1 else windows[c].at[part(r - 1)]
        return remote(
            source, windows[c].at[part(r)], short_send.at[r - 1], short_recv.at[c, r - 1], {"blk": following}
        )

    def long_hop(c, r):
        u = SPREAD_SHORT + c

        def landing(r):
            return relays[c].at[r - 1] if r <= ROW - REACH else windows[u].at[part(ROW + 1 - r)]

        source = a_ref.at[:, span(u)] if r == 1 else landing(r - 1)
        return remote(
            source, landing(r), long_send.at[r - 1], long_recv.at[c, r - 1], {"blk": beyond if r == 1 else previous}
        )

    def give_own(e):
        to = others[e - 1]
        return remote(a_ref.at[to], own_ref.at[t], own_send.at[e - 1], own_recv.at[e - 1], tile_place(to, cores))

    def give(e, at):
        to = others[e - 1]
        return remote(
            picked_ref.at[to, at], theirs_ref.at[t, at], out_send.at[e - 1], out_recv.at[e - 1], tile_place(to, cores)
        )

    start = (p - REACH) * blocks
    total = n * blocks
    index = []
    for k in range(blocks):
        for j in range(SLOTS):
            w = pred_ref[k, j] - start
            w = jnp.where(w < 0, w + total, w)
            w = jnp.where(w >= total, w - total, w)
            index.append(jnp.clip(w, 0, (REACH + 1) * blocks - 1))

    def pick(u):
        for k in range(blocks):
            for j in range(SLOTS):
                picked_ref[k, span(u), j * R : (j + 1) * R] = windows[u][index[k * SLOTS + j]]

    def copy_own():
        for u in range(chunks):
            windows[u][REACH * blocks :] = a_ref[:, span(u)]
        own_ref[t] = a_ref[t]

    begun = False
    for is_long, c, r in order(SPREAD_SHORT, SPREAD_LONG, 2.4, 2.8, 2.4, 2.8, 1):
        hop, last = (long_hop, ROW) if is_long else (short_hop, REACH)
        if r > 1:
            if not begun:
                for e in range(1, peers):
                    give_own(e).start()
                copy_own()
                begun = True
            hop(c, r - 1).wait_recv()
        if r <= last:
            hop(c, r).start()
        else:
            u = SPREAD_SHORT + c if is_long else c
            pick(u)
            for e in range(1, peers):
                give(e, span(u)).start()
    theirs_ref[t] = picked_ref[t]
    for e in range(1, peers):
        give_own(e).wait_recv()
        give(e, slice(0, members)).wait_recv()
    for r in range(1, REACH + 1):
        width = SPREAD_SHORT * rows
        remote(
            a_ref.at[:, :width], a_ref.at[:, :width], short_send.at[r - 1], short_recv.at[0, 0], {"blk": following}
        ).wait_send()
    for r in range(1, ROW + 1):
        width = SPREAD_LONG * rows
        remote(
            a_ref.at[:, :width], a_ref.at[:, :width], long_send.at[r - 1], long_recv.at[0, 0], {"blk": following}
        ).wait_send()
    for e in range(1, peers):
        give_own(e).wait_send()
        give(e, slice(0, members)).wait_send()


def spread(predecessors, anomalies, peers):
    blocks, members, _ = anomalies.shape
    chunks = SPREAD_SHORT + SPREAD_LONG
    rows = members // chunks
    bf16 = jnp.bfloat16
    return pl.pallas_call(
        spread_kernel,
        out_shape=(
            jax.ShapeDtypeStruct((blocks, members, SLOTS * R), bf16),
            jax.ShapeDtypeStruct((peers, members, SLOTS * R), bf16),
            jax.ShapeDtypeStruct((peers, members, R), bf16),
        ),
        in_specs=[SM, VM],
        out_specs=(VM, VM, VM),
        scratch_shapes=[pltpu.VMEM(((REACH + 1) * blocks, rows, R), bf16) for _ in range(chunks)]
        + [pltpu.VMEM((ROW - REACH, blocks, rows, R), bf16) for _ in range(SPREAD_LONG)]
        + [dma((REACH,)), dma((SPREAD_SHORT, REACH)), dma((ROW,)), dma((SPREAD_LONG, ROW))]
        + [dma((peers - 1,)) for _ in range(4)],
        compiler_params=pltpu.CompilerParams(collective_id=0, has_side_effects=True),
        name="spread",
    )(predecessors, anomalies)


def invert_block(d):
    sub = lax.broadcasted_iota(jnp.int32, (8, 128), 0)
    lane = lax.broadcasted_iota(jnp.int32, (8, 128), 1)
    groups = d.shape[0] // 8
    rows = [d[8 * g : 8 * g + 8, :] for g in range(groups)]

    def across(v, c):
        return jnp.broadcast_to(v[:, c : c + 1], (8, 128))

    def down(v, s):
        return jnp.broadcast_to(v[s : s + 1, :], (8, 128))

    for q in range(groups):
        p = rows[q]
        t = [across(p, 8 * q + c) for c in range(8)]
        for s in range(8):
            inv = 1.0 / down(t[s], s)
            at = lane == 8 * q + s
            row = jnp.where(at, inv, down(p, s) * inv)
            p = jnp.where(sub == s, row, jnp.where(at, 0.0, p) - t[s] * row)
            for c in range(s + 1, 8):
                n = down(t[c], s) * inv
                t[c] = jnp.where(sub == s, n, t[c] - t[s] * n)
        b = [down(p, s) for s in range(8)]
        panel = (lane >= 8 * q) & (lane < 8 * q + 8)
        for g in range(groups):
            if g == q:
                continue
            old = rows[g]
            new = jnp.where(panel, 0.0, old)
            for s in range(8):
                new = new - across(old, 8 * q + s) * b[s]
            rows[g] = new
        rows[q] = p
    return jnp.concatenate(rows, axis=0)


def mm(a, b, dims=((1,), (0,))):
    return lax.dot_general(a, b, (dims, ((), ())), precision=HI, preferred_element_type=jnp.float32)


def solve_kernel(x_ref, own_ref, coef_ref, var_ref, s_ref, w_ref):
    members = x_ref.shape[0]
    x, own = x_ref[...], own_ref[...]
    dims = (((0,), (0,)), ((), ()))
    s_ref[...] = lax.dot_general(
        x, jnp.concatenate([x, own], axis=1), dims, preferred_element_type=jnp.float32
    ) * (1.0 / members)
    eye = lax.broadcasted_iota(jnp.int32, (R, R), 0) == lax.broadcasted_iota(jnp.int32, (R, R), 1)
    ridge = jnp.where(eye, RIDGE_TERM, 0.0)

    def step(i, carry):
        lo = pl.multiple_of(i * R, R)
        w_ref[i] = invert_block(s_ref[pl.ds(lo, R), pl.ds(lo, R)] + ridge)
        for c in range(4):
            @pl.when(i == c)
            def _(c=c):
                a, z = c * R, (c + 1) * R
                w = w_ref[c]
                u = mm(w, s_ref[a:z, z:])
                if c < 3:
                    s_ref[z:, z:] -= mm(s_ref[a:z, z : 4 * R], u, ((0,), (0,)))
                s_ref[a:z, z:] = u
        return carry

    lax.fori_loop(0, 4, step, 0)
    for c in range(2, -1, -1):
        a, z = c * R, (c + 1) * R
        s_ref[a:z, 4 * R :] -= mm(s_ref[a:z, z : 4 * R], s_ref[z : 4 * R, 4 * R :])
    coef = s_ref[:, 4 * R :].astype(jnp.bfloat16)
    coef_ref[...] = coef
    resid = own.astype(jnp.float32) - jnp.dot(x, coef, preferred_element_type=jnp.float32)
    total = jnp.sum(resid * resid, axis=0, keepdims=True)
    var_ref[...] = jnp.broadcast_to(total * (1.0 / members) + EPSILON, var_ref.shape)


def solve(x, own):
    return pl.pallas_call(
        solve_kernel,
        out_shape=(jax.ShapeDtypeStruct((512, 128), jnp.bfloat16), jax.ShapeDtypeStruct((8, 128), jnp.float32)),
        in_specs=[VM, VM],
        out_specs=(VM, VM),
        scratch_shapes=[pltpu.VMEM((512, 640), jnp.float32), pltpu.VMEM((4, 128, 128), jnp.float32)],
        name="solve",
    )(x, own)


def finish_kernel(
    table_ref, picked_ref, a_ref, coef_ref, var_ref, out_ref, vars_ref,
    all_ref, landed_vars, terms, short_landed, short_staged, long_landed, long_staged,
    send, recv, var_send, var_recv, short_send, short_recv, long_send, long_recv,
):
    p, n, t, peers, cores = places()
    blocks, members, _ = out_ref.shape
    chunks = COLLECT_SHORT + COLLECT_LONG
    rows = members // chunks
    following, previous = lax.rem(p + 1, n), lax.rem(p + n - 1, n)
    beyond, behind = lax.rem(p + ROW, n), lax.rem(p + n - ROW, n)
    chips = peers // cores
    x, core = lax.axis_index("tile_0"), lax.axis_index("tile_1")
    right, left, far = lax.rem(x + 1, chips), lax.rem(x + chips - 1, chips), lax.rem(x + 2, chips)
    other = 1 - core
    others = [lax.rem(t + e, peers) for e in range(1, peers)]
    meet([tile_place(o, cores) for o in others] + [{"blk": b} for b in (following, previous, beyond, behind)])

    half = coef_ref.shape[0] // 2
    low, high = slice(0, half), slice(half, 2 * half)

    def variance(e):
        to = tile_place(others[e - 1], cores)
        return remote(var_ref, landed_vars.at[t], var_send.at[e - 1], var_recv.at[e - 1], to)

    def pass_on(i, source, chip, here, part, where):
        view = all_ref.at[chip * cores + here, part]
        return remote(view if source is None else source.at[part], view, send.at[i], recv.at[i], where)

    low_right = pass_on(0, coef_ref, x, core, low, {"tile_0": right})
    high_left = pass_on(1, coef_ref, x, core, high, {"tile_0": left})
    high_right = pass_on(2, coef_ref, x, core, high, {"tile_0": right})
    low_left = pass_on(3, coef_ref, x, core, low, {"tile_0": left})
    own_across = pass_on(4, coef_ref, x, core, slice(0, 2 * half), {"tile_1": other})
    on_right = pass_on(5, None, left, core, low, {"tile_0": right})
    on_left = pass_on(6, None, right, core, high, {"tile_0": left})

    def across(i, chip, part):
        return pass_on(i, None, chip, core, part, {"tile_1": other})

    for copy in (low_right, high_left, high_right, low_left, own_across):
        copy.start()
    for e in range(1, peers):
        variance(e).start()
    all_ref[t] = coef_ref[...]
    landed_vars[t] = var_ref[...]
    terms[SLOTS * blocks] = jnp.zeros_like(terms[SLOTS * blocks])

    def weigh(k):
        coef = all_ref[k]
        resid = a_ref[k].astype(jnp.float32) - jnp.dot(picked_ref[k], coef, preferred_element_type=jnp.float32)
        weighted = (resid / landed_vars[k, 0:1, :]).astype(jnp.bfloat16)
        out_ref[k] = weighted.astype(jnp.float32)
        back = lax.dot_general(weighted, coef, (((1,), (1,)), ((), ())), preferred_element_type=jnp.float32)
        for j in range(SLOTS):
            terms[k * SLOTS + j] = back[:, j * R : (j + 1) * R]

    weigh(t)
    for e in range(1, peers):
        variance(e).wait_recv()
    steps = [
        (low_right, on_right, across(7, left, low)),
        (high_left, on_left, across(8, right, high)),
        (high_right, None, across(9, left, high)),
        (low_left, None, across(10, right, low)),
        (on_right, None, across(11, far, low)),
        (on_left, None, across(12, far, high)),
    ]
    for i, (arrived, forward, sideways) in enumerate(steps):
        arrived.wait_recv()
        if forward is not None:
            forward.start()
        sideways.start()
        if i == 1:
            own_across.wait_recv()
            weigh(x * cores + other)
        if i == 3:
            weigh(left * cores + core)
            weigh(right * cores + core)
    weigh(far * cores + core)
    for first, second, chip in ((0, 2, left), (1, 3, right), (4, 5, far)):
        steps[first][2].wait_recv()
        steps[second][2].wait_recv()
        weigh(chip * cores + other)
    for k in range(blocks):
        vars_ref[k : k + 1, :] = landed_vars[k, 0:1, :]

    def span(u):
        return slice(u * rows, (u + 1) * rows)

    def terms_for(block, u):
        slot = table_ref[block * blocks]
        total = terms[slot, span(u)]
        for k in range(1, blocks):
            total = total + terms[table_ref[block * blocks + k], span(u)]
        return total

    def short_hop(c, r):
        source = short_staged.at[c, r - 1]
        return remote(source, short_landed.at[c, r - 1], short_send.at[r - 1], short_recv.at[c, r - 1], {"blk": previous})

    def long_hop(c, r):
        source = long_staged.at[c, r - 1] if r <= REACH else long_landed.at[c, r - 2]
        where = behind if r == ROW else following
        return remote(source, long_landed.at[c, r - 1], long_send.at[r - 1], long_recv.at[c, r - 1], {"blk": where})

    def add(u, distance, arrived, staged):
        for i in range(blocks):
            total = terms_for((REACH - distance) * blocks + i, u)
            if arrived is not None:
                total = total + arrived[i].astype(jnp.float32)
            staged[i] = total.astype(jnp.bfloat16)

    def close(u, arrived):
        for i in range(blocks):
            total = terms_for(REACH * blocks + i, u) + arrived[i].astype(jnp.float32)
            out_ref[i, span(u)] = out_ref[i, span(u)] - total

    for is_long, c, r in order(COLLECT_SHORT, COLLECT_LONG, 0.7, 3.5, 0.7, 2.8, 1):
        hop, last = (long_hop, ROW) if is_long else (short_hop, REACH)
        landed, staged = (long_landed, long_staged) if is_long else (short_landed, short_staged)
        u = COLLECT_SHORT + c if is_long else c
        if r > 1:
            hop(c, r - 1).wait_recv()
        if r <= REACH:
            add(u, r if is_long else REACH + 1 - r, landed.at[c, r - 2] if r > 1 else None, staged.at[c, r - 1])
        if r <= last:
            hop(c, r).start()
        else:
            close(u, landed.at[c, r - 2])
    for copy in (low_right, high_left, high_right, low_left, own_across, on_right, on_left):
        copy.wait_send()
    for _, _, sideways in steps:
        sideways.wait_send()
    for e in range(1, peers):
        variance(e).wait_send()
    for r in range(1, REACH + 1):
        view = short_landed.at[:, r - 1]
        remote(view, view, short_send.at[r - 1], short_recv.at[0, 0], {"blk": previous}).wait_send()
    for r in range(1, ROW + 1):
        view = long_landed.at[:, r - 1]
        remote(view, view, long_send.at[r - 1], long_recv.at[0, 0], {"blk": previous}).wait_send()


def finish(table, picked, anomalies, coef, var, peers):
    blocks, members, _ = anomalies.shape
    rows = members // (COLLECT_SHORT + COLLECT_LONG)
    f32, bf16 = jnp.float32, jnp.bfloat16
    short = pltpu.VMEM((COLLECT_SHORT, REACH, blocks, rows, R), bf16)
    return pl.pallas_call(
        finish_kernel,
        out_shape=(
            jax.ShapeDtypeStruct((blocks, members, R), f32),
            jax.ShapeDtypeStruct((blocks, R), f32),
        ),
        in_specs=[SM, VM, VM, VM, VM],
        out_specs=(VM, VM),
        scratch_shapes=[
            pltpu.VMEM((peers,) + coef.shape, bf16),
            pltpu.VMEM((peers,) + var.shape, f32),
            pltpu.VMEM((SLOTS * blocks + 1, members, R), f32),
            short,
            short,
            pltpu.VMEM((COLLECT_LONG, ROW, blocks, rows, R), bf16),
            pltpu.VMEM((COLLECT_LONG, REACH, blocks, rows, R), bf16),
            dma((13,)),
            dma((13,)),
            dma((peers - 1,)),
            dma((peers - 1,)),
            dma((REACH,)),
            dma((COLLECT_SHORT, REACH)),
            dma((ROW,)),
            dma((COLLECT_LONG, ROW)),
        ],
        compiler_params=pltpu.CompilerParams(collective_id=1, has_side_effects=True),
        name="finish",
    )(table, picked, anomalies, coef, var)


def local(anomalies, predecessors):
    blocks, members, _ = anomalies.shape
    peers = lax.axis_size(TILE)
    picked, theirs, own = spread(predecessors, anomalies, peers)
    coef, var = solve(theirs.reshape(peers * members, SLOTS * R), own.reshape(peers * members, R))
    total_blocks = blocks * lax.axis_size("blk")
    window_start = (lax.axis_index("blk") - REACH) * blocks
    index = jnp.mod(predecessors - window_start, total_blocks)
    slots = jnp.arange((REACH + 1) * blocks, dtype=jnp.int32)[:, None]
    table = jnp.full(((REACH + 1) * blocks, blocks), SLOTS * blocks, jnp.int32)
    for j in range(SLOTS):
        table = jnp.where(index[None, :, j] == slots, jnp.arange(blocks, dtype=jnp.int32)[None] * SLOTS + j, table)
    applied, variances = finish(table.reshape(-1), picked, anomalies, coef, var, peers)
    return applied, coef[None], variances


def solution(mesh):
    chips = mesh.shape["tile"] // 2
    split = Mesh(mesh.devices.reshape(mesh.shape["blk"], chips, 2), ("blk", "tile_0", "tile_1"))
    return jax.shard_map(
        local,
        mesh=split,
        in_specs=(P("blk", TILE, None), P("blk", None)),
        out_specs=(P("blk", TILE, None), P(BLK_TILE, None, None), P("blk", None)),
        check_vma=False,
    )
```

time: 174 us -> 159 us (0.914)
  Pallas kernels: 168 us -> 152 us
  local copies, waits for them, and re-layouts: 2.11 us -> 4.89 us
  other arithmetic: 2.71 us -> 0.72 us
    pallas_call x3 -> x1, Pallas kernels: 70.8 us -> 56.8 us  [finish(): pl.pallas_call(finish_kernel, out_shape=(jax.ShapeDtypeStruct((blocks, me...]
    unnamed x3 -> x5, local copies, waits for them, and re-layouts: 0.76 us -> 4.21 us
    sub x1 -> x0, other arithmetic: 2.1 us -> none  [local(): applied = own - collect(near, far).astype(jnp.float32)]
    pallas_call x1, Pallas kernels: 71.7 us -> 69.9 us  [spread(): pl.pallas_call(spread_kernel, out_shape=(jax.ShapeDtypeStruct((blocks, me...]
where the time goes in v2:
time: 159 us; the launch traced here: 158 us
  Pallas kernels  152 us (96%)
  local copies, waits for them, and re-layouts  4.89 us (3%)
    pallas_call x1, Pallas kernels, spread(): pl.pallas_call(spread_kernel, out_shape=(jax.ShapeDtypeStruct((blocks, me...  69.9 us
    pallas_call x1, Pallas kernels, finish(): pl.pallas_call(finish_kernel, out_shape=(jax.ShapeDtypeStruct((blocks, me...  56.8 us
    pallas_call x1, Pallas kernels, solve(): pl.pallas_call(solve_kernel, out_shape=(jax.ShapeDtypeStruct((512, 128),...  25.3 us
    unnamed x5, local copies, waits for them, and re-layouts  4.21 us

profile of v2, /device:TPU:1, one launch (start us, length us, event | category | flops | bytes accessed | tf_op | source)
XLA Modules:
  0.0 158.3 jit_solution(16342648767535651167)
XLA Ops:
  0.7 0.7 add_select_fusion
  1.4 1.3 copy.6.pred_ref
  2.7 0.7 reshape.53.table_ref
  3.4 69.9 %spread.1 = (bf16[8,256,512]{2,1,0:T(8,128)(2,1)}, bf16[8,256,512]{2,1,0:T(8,128)(2,1)}, bf16[8,256,128]{2,1,0:T(8,128)(2,1)}) custom-call(s32[8,4]{1,0:T(8,128)} %copy.6.pred_ref, bf16[8,256,128]{2,1,0:T(8,128)(2,1)} %a_ref.3), custom_call_target="tpu_custom_call" | custom-call | tf_op jit(solution)/shard_map/spread/pallas_call | solution.py:170
  73.3 25.3 %solve.1 = (bf16[512,128]{1,0:T(8,128)(2,1)}, f32[8,128]{1,0:T(8,128)}) custom-call(bf16[2048,512]{1,0:T(8,128)(2,1)} %bitcast.11, bf16[2048,128]{1,0:T(8,128)(2,1)} %bitcast.12), custom_call_target="tpu_custom_call" | custom-call | tf_op jit(solution)/shard_map/solve/pallas_call | solution.py:265
  98.6 56.8 %finish.1 = (f32[8,256,128]{2,1,0:T(8,128)}, f32[8,128]{1,0:T(8,128)}) custom-call(s32[320]{0:T(512)} %reshape.53.table_ref, bf16[8,256,512]{2,1,0:T(8,128)(2,1)} %get-tuple-element.10.picked_ref, bf16[8,256,128]{2,1,0:T(8,128)(2,1)} %a_ref.3, bf16[512,128]{1,0:T(8,128)(2,1)} %get-tuple-element.13.coef_ref, f32[8,128]{1,0:T(8,128)} %get-tuple-element.14.var_ref), custom_call_target="tpu_custom_call" | custom-call | tf_op jit(solution)/shard_map/finish/pallas_call | solution.py:424
  155.4 0.0 copy-start
  155.4 2.3 %copy.9 = f32[8,256,128]{2,1,0:T(8,128)} copy(f32[8,256,128]{2,1,0:T(8,128)} %get-tuple-element.28) | data formatting | bytes 2097152
  157.7 0.0 copy-done
  157.7 0.6 copy.10
  (4 shorter events, 0.0 us)
Async XLA Ops:
  155.4 2.3 %copy-start = (f32[8,128]{1,0:T(8,128)S(1)}, f32[8,128]{1,0:T(8,128)}, u32[]{:S(2)}) copy-start(f32[8,128]{1,0:T(8,128)} %get-tuple-element.30) | copy-start | bytes 12292

commit v3 on v2

--- a/solution.py
+++ b/solution.py
@@ -16,13 +16,19 @@
 R = 128
 SLOTS = 4
 REACH = 4
-ROW = 8
+JUMP = 5
 VM = pl.BlockSpec(memory_space=pltpu.VMEM)
 SM = pl.BlockSpec(memory_space=pltpu.SMEM)
 dma = pltpu.SemaphoreType.DMA
 
 SPREAD_SHORT, SPREAD_LONG = 11, 5
 COLLECT_SHORT, COLLECT_LONG = 5, 3
+SPREAD_ORDER = (
+    11, 12, 0, 3, 5, 13, 1, 0, 10, 7, 14, 8, 2, 1, 11, 9, 0, 15, 12, 4, 2, 5, 3, 6,
+    13, 1, 11, 7, 14, 12, 0, 2, 4, 13, 9, 15, 14, 6, 12, 1, 11, 15, 13, 3, 5, 0, 12, 14,
+    2, 4, 8, 11, 9, 6, 1, 13, 12, 5, 2, 11, 3, 4, 7, 13, 15, 9, 6, 5, 8, 10, 4, 15,
+    7, 14, 3, 9, 6, 10, 15, 8, 14, 10, 7, 10, 8,
+)
 
 
 def remote(src, dst, send_sem, recv_sem, where):
@@ -48,16 +54,37 @@
     pl.semaphore_wait(barrier, len(targets))
 
 
+def window_index(pred_ref, p, n):
+    blocks = pred_ref.shape[1]
+    start, total = (p - REACH) * blocks, n * blocks
+    index = []
+    for k in range(blocks):
+        for j in range(SLOTS):
+            w = pred_ref[j, k] - start
+            w = jnp.where(w < 0, w + total, w)
+            w = jnp.where(w >= total, w - total, w)
+            index.append(jnp.clip(w, 0, (REACH + 1) * blocks - 1))
+    return index
+
+
 def order(short, long, short_step, short_hop, long_step, long_hop, closing):
     plan = []
     for is_long, chunks, hops, step, hop in (
         (False, short, REACH, short_step, short_hop),
-        (True, long, ROW, long_step, long_hop),
+        (True, long, JUMP, long_step, long_hop),
     ):
         for c in range(chunks):
             for r in range(1, hops + 1 + closing):
                 plan.append((step * c + hop * (r - 1), is_long, c, r))
     return [entry[1:] for entry in sorted(plan)]
+
+
+def listed_order(chunks, short):
+    rounds, plan = {}, []
+    for u in chunks:
+        rounds[u] = rounds.get(u, 0) + 1
+        plan.append((u >= short, u - short if u >= short else u, rounds[u]))
+    return plan
 
 
 def spread_kernel(pred_ref, a_ref, picked_ref, theirs_ref, own_ref, *rest):
@@ -69,7 +96,7 @@
     blocks, members = a_ref.shape[0], a_ref.shape[1]
     rows = members // chunks
     following, previous = lax.rem(p + 1, n), lax.rem(p + n - 1, n)
-    beyond, behind = lax.rem(p + ROW, n), lax.rem(p + n - ROW, n)
+    beyond, behind = lax.rem(p + JUMP, n), lax.rem(p + n - JUMP, n)
     others = [lax.rem(t + e, peers) for e in range(1, peers)]
     meet([{"blk": b} for b in (following, previous, beyond, behind)] + [tile_place(o, cores) for o in others])
 
@@ -89,7 +116,7 @@
         u = SPREAD_SHORT + c
 
         def landing(r):
-            return relays[c].at[r - 1] if r <= ROW - REACH else windows[u].at[part(ROW + 1 - r)]
+            return relays[c].at[r - 1] if r <= JUMP - REACH else windows[u].at[part(JUMP + 1 - r)]
 
         source = a_ref.at[:, span(u)] if r == 1 else landing(r - 1)
         return remote(
@@ -106,15 +133,7 @@
             picked_ref.at[to, at], theirs_ref.at[t, at], out_send.at[e - 1], out_recv.at[e - 1], tile_place(to, cores)
         )
 
-    start = (p - REACH) * blocks
-    total = n * blocks
-    index = []
-    for k in range(blocks):
-        for j in range(SLOTS):
-            w = pred_ref[k, j] - start
-            w = jnp.where(w < 0, w + total, w)
-            w = jnp.where(w >= total, w - total, w)
-            index.append(jnp.clip(w, 0, (REACH + 1) * blocks - 1))
+    index = window_index(pred_ref, p, n)
 
     def pick(u):
         for k in range(blocks):
@@ -127,8 +146,8 @@
         own_ref[t] = a_ref[t]
 
     begun = False
-    for is_long, c, r in order(SPREAD_SHORT, SPREAD_LONG, 2.4, 2.8, 2.4, 2.8, 1):
-        hop, last = (long_hop, ROW) if is_long else (short_hop, REACH)
+    for is_long, c, r in listed_order(SPREAD_ORDER, SPREAD_SHORT):
+        hop, last = (long_hop, JUMP) if is_long else (short_hop, REACH)
         if r > 1:
             if not begun:
                 for e in range(1, peers):
@@ -152,7 +171,7 @@
         remote(
             a_ref.at[:, :width], a_ref.at[:, :width], short_send.at[r - 1], short_recv.at[0, 0], {"blk": following}
         ).wait_send()
-    for r in range(1, ROW + 1):
+    for r in range(1, JUMP + 1):
         width = SPREAD_LONG * rows
         remote(
             a_ref.at[:, :width], a_ref.at[:, :width], long_send.at[r - 1], long_recv.at[0, 0], {"blk": following}
@@ -177,8 +196,8 @@
         in_specs=[SM, VM],
         out_specs=(VM, VM, VM),
         scratch_shapes=[pltpu.VMEM(((REACH + 1) * blocks, rows, R), bf16) for _ in range(chunks)]
-        + [pltpu.VMEM((ROW - REACH, blocks, rows, R), bf16) for _ in range(SPREAD_LONG)]
-        + [dma((REACH,)), dma((SPREAD_SHORT, REACH)), dma((ROW,)), dma((SPREAD_LONG, ROW))]
+        + [pltpu.VMEM((JUMP - REACH, blocks, rows, R), bf16) for _ in range(SPREAD_LONG)]
+        + [dma((REACH,)), dma((SPREAD_SHORT, REACH)), dma((JUMP,)), dma((SPREAD_LONG, JUMP))]
         + [dma((peers - 1,)) for _ in range(4)],
         compiler_params=pltpu.CompilerParams(collective_id=0, has_side_effects=True),
         name="spread",
@@ -226,7 +245,14 @@
     return lax.dot_general(a, b, (dims, ((), ())), precision=HI, preferred_element_type=jnp.float32)
 
 
-def solve_kernel(x_ref, own_ref, coef_ref, var_ref, s_ref, w_ref):
+def solve_kernel(pred_ref, x_ref, own_ref, coef_ref, var_ref, table_ref, s_ref):
+    blocks = pred_ref.shape[1]
+    for i in range(table_ref.shape[0]):
+        table_ref[i] = SLOTS * blocks
+    index = window_index(pred_ref, lax.axis_index("blk"), lax.axis_size("blk"))
+    for k in range(blocks):
+        for j in range(SLOTS):
+            table_ref[index[k * SLOTS + j] * blocks + k] = k * SLOTS + j
     members = x_ref.shape[0]
     x, own = x_ref[...], own_ref[...]
     dims = (((0,), (0,)), ((), ()))
@@ -236,21 +262,17 @@
     eye = lax.broadcasted_iota(jnp.int32, (R, R), 0) == lax.broadcasted_iota(jnp.int32, (R, R), 1)
     ridge = jnp.where(eye, RIDGE_TERM, 0.0)
 
-    def step(i, carry):
-        lo = pl.multiple_of(i * R, R)
-        w_ref[i] = invert_block(s_ref[pl.ds(lo, R), pl.ds(lo, R)] + ridge)
-        for c in range(4):
-            @pl.when(i == c)
-            def _(c=c):
-                a, z = c * R, (c + 1) * R
-                w = w_ref[c]
-                u = mm(w, s_ref[a:z, z:])
-                if c < 3:
-                    s_ref[z:, z:] -= mm(s_ref[a:z, z : 4 * R], u, ((0,), (0,)))
-                s_ref[a:z, z:] = u
-        return carry
-
-    lax.fori_loop(0, 4, step, 0)
+    diag = s_ref[:R, :R]
+    for c in range(4):
+        a, z = c * R, (c + 1) * R
+        w = invert_block(diag + ridge)
+        if c < 3:
+            side = s_ref[a:z, z : z + R]
+            diag = s_ref[z : z + R, z : z + R] - mm(side, mm(w, side), ((0,), (0,)))
+        u = mm(w, s_ref[a:z, z:])
+        if c < 3:
+            s_ref[z:, z:] -= mm(s_ref[a:z, z : 4 * R], u, ((0,), (0,)))
+        s_ref[a:z, z:] = u
     for c in range(2, -1, -1):
         a, z = c * R, (c + 1) * R
         s_ref[a:z, 4 * R :] -= mm(s_ref[a:z, z : 4 * R], s_ref[z : 4 * R, 4 * R :])
@@ -261,15 +283,20 @@
     var_ref[...] = jnp.broadcast_to(total * (1.0 / members) + EPSILON, var_ref.shape)
 
 
-def solve(x, own):
+def solve(predecessors, x, own):
+    slots = (REACH + 1) * predecessors.shape[1] ** 2
     return pl.pallas_call(
         solve_kernel,
-        out_shape=(jax.ShapeDtypeStruct((512, 128), jnp.bfloat16), jax.ShapeDtypeStruct((8, 128), jnp.float32)),
-        in_specs=[VM, VM],
-        out_specs=(VM, VM),
-        scratch_shapes=[pltpu.VMEM((512, 640), jnp.float32), pltpu.VMEM((4, 128, 128), jnp.float32)],
+        out_shape=(
+            jax.ShapeDtypeStruct((512, 128), jnp.bfloat16),
+            jax.ShapeDtypeStruct((8, 128), jnp.float32),
+            jax.ShapeDtypeStruct((slots,), jnp.int32),
+        ),
+        in_specs=[SM, VM, VM],
+        out_specs=(VM, VM, SM),
+        scratch_shapes=[pltpu.VMEM((512, 640), jnp.float32)],
         name="solve",
-    )(x, own)
+    )(predecessors, x, own)
 
 
 def finish_kernel(
@@ -282,7 +309,7 @@
     chunks = COLLECT_SHORT + COLLECT_LONG
     rows = members // chunks
     following, previous = lax.rem(p + 1, n), lax.rem(p + n - 1, n)
-    beyond, behind = lax.rem(p + ROW, n), lax.rem(p + n - ROW, n)
+    beyond, behind = lax.rem(p + JUMP, n), lax.rem(p + n - JUMP, n)
     chips = peers // cores
     x, core = lax.axis_index("tile_0"), lax.axis_index("tile_1")
     right, left, far = lax.rem(x + 1, chips), lax.rem(x + chips - 1, chips), lax.rem(x + 2, chips)
@@ -375,7 +402,7 @@
 
     def long_hop(c, r):
         source = long_staged.at[c, r - 1] if r <= REACH else long_landed.at[c, r - 2]
-        where = behind if r == ROW else following
+        where = behind if r == JUMP else following
         return remote(source, long_landed.at[c, r - 1], long_send.at[r - 1], long_recv.at[c, r - 1], {"blk": where})
 
     def add(u, distance, arrived, staged):
@@ -390,8 +417,8 @@
             total = terms_for(REACH * blocks + i, u) + arrived[i].astype(jnp.float32)
             out_ref[i, span(u)] = out_ref[i, span(u)] - total
 
-    for is_long, c, r in order(COLLECT_SHORT, COLLECT_LONG, 0.7, 3.5, 0.7, 2.8, 1):
-        hop, last = (long_hop, ROW) if is_long else (short_hop, REACH)
+    for is_long, c, r in order(COLLECT_SHORT, COLLECT_LONG, 0.87, 7.9, 2.84, 6.02, 1):
+        hop, last = (long_hop, JUMP) if is_long else (short_hop, REACH)
         landed, staged = (long_landed, long_staged) if is_long else (short_landed, short_staged)
         u = COLLECT_SHORT + c if is_long else c
         if r > 1:
@@ -411,7 +438,7 @@
     for r in range(1, REACH + 1):
         view = short_landed.at[:, r - 1]
         remote(view, view, short_send.at[r - 1], short_recv.at[0, 0], {"blk": previous}).wait_send()
-    for r in range(1, ROW + 1):
+    for r in range(1, JUMP + 1):
         view = long_landed.at[:, r - 1]
         remote(view, view, long_send.at[r - 1], long_recv.at[0, 0], {"blk": previous}).wait_send()
 
@@ -435,7 +462,7 @@
             pltpu.VMEM((SLOTS * blocks + 1, members, R), f32),
             short,
             short,
-            pltpu.VMEM((COLLECT_LONG, ROW, blocks, rows, R), bf16),
+            pltpu.VMEM((COLLECT_LONG, JUMP, blocks, rows, R), bf16),
             pltpu.VMEM((COLLECT_LONG, REACH, blocks, rows, R), bf16),
             dma((13,)),
             dma((13,)),
@@ -443,8 +470,8 @@
             dma((peers - 1,)),
             dma((REACH,)),
             dma((COLLECT_SHORT, REACH)),
-            dma((ROW,)),
-            dma((COLLECT_LONG, ROW)),
+            dma((JUMP,)),
+            dma((COLLECT_LONG, JUMP)),
         ],
         compiler_params=pltpu.CompilerParams(collective_id=1, has_side_effects=True),
         name="finish",
@@ -454,16 +481,10 @@
 def local(anomalies, predecessors):
     blocks, members, _ = anomalies.shape
     peers = lax.axis_size(TILE)
-    picked, theirs, own = spread(predecessors, anomalies, peers)
-    coef, var = solve(theirs.reshape(peers * members, SLOTS * R), own.reshape(peers * members, R))
-    total_blocks = blocks * lax.axis_size("blk")
-    window_start = (lax.axis_index("blk") - REACH) * blocks
-    index = jnp.mod(predecessors - window_start, total_blocks)
-    slots = jnp.arange((REACH + 1) * blocks, dtype=jnp.int32)[:, None]
-    table = jnp.full(((REACH + 1) * blocks, blocks), SLOTS * blocks, jnp.int32)
-    for j in range(SLOTS):
-        table = jnp.where(index[None, :, j] == slots, jnp.arange(blocks, dtype=jnp.int32)[None] * SLOTS + j, table)
-    applied, variances = finish(table.reshape(-1), picked, anomalies, coef, var, peers)
+    listed = predecessors.T
+    picked, theirs, own = spread(listed, anomalies, peers)
+    coef, var, table = solve(listed, theirs.reshape(peers * members, SLOTS * R), own.reshape(peers * members, R))
+    applied, variances = finish(table, picked, anomalies, coef, var, peers)
     return applied, coef[None], variances
 
 

time: 159 us -> 139 us (0.87)
  Pallas kernels: 152 us -> 135 us
  local copies, waits for them, and re-layouts: 4.89 us -> 2.87 us
    pallas_call x1, Pallas kernels: 69.9 us -> 62.1 us  [spread(): pl.pallas_call(spread_kernel, out_shape=(jax.ShapeDtypeStruct((blocks, me...]
    pallas_call x1, Pallas kernels: 56.8 us -> 50.1 us  [finish(): pl.pallas_call(finish_kernel, out_shape=(jax.ShapeDtypeStruct((blocks, me...]
    pallas_call x1, Pallas kernels: 25.3 us -> 23.2 us  [solve(): pl.pallas_call(solve_kernel, out_shape=(jax.ShapeDtypeStruct((512, 128),...]
    unnamed x5 -> x4, local copies, waits for them, and re-layouts: 4.21 us -> 2.87 us
where the time goes in v3:
time: 139 us
  Pallas kernels  135 us (97%)
  local copies, waits for them, and re-layouts  2.87 us (2%)
    pallas_call x1, Pallas kernels, spread(): pl.pallas_call(spread_kernel, out_shape=(jax.ShapeDtypeStruct((blocks, me...  62.1 us
    pallas_call x1, Pallas kernels, finish(): pl.pallas_call(finish_kernel, out_shape=(jax.ShapeDtypeStruct((blocks, me...  50.1 us
    pallas_call x1, Pallas kernels, solve(): pl.pallas_call(solve_kernel, out_shape=(jax.ShapeDtypeStruct((512, 128),...  23.2 us
    unnamed x4, local copies, waits for them, and re-layouts  2.87 us

profile of v3, /device:TPU:1, one launch (start us, length us, event | category | flops | bytes accessed | tf_op | source)
XLA Modules:
  0.0 139.0 jit_solution(4667057741330540355)
XLA Ops:
  0.6 62.1 %spread.1 = (bf16[8,256,512]{2,1,0:T(8,128)(2,1)}, bf16[8,256,512]{2,1,0:T(8,128)(2,1)}, bf16[8,256,128]{2,1,0:T(8,128)(2,1)}) custom-call(s32[4,8]{1,0:T(4,128)} %bitcast.7, bf16[8,256,128]{2,1,0:T(8,128)(2,1)} %a_ref.3), custom_call_target="tpu_custom_call" | custom-call | tf_op jit(solution)/shard_map/spread/pallas_call | solution.py:189
  62.8 23.2 %solve.1 = (bf16[512,128]{1,0:T(8,128)(2,1)}, f32[8,128]{1,0:T(8,128)}, s32[320]{0:T(512)}) custom-call(s32[4,8]{1,0:T(4,128)} %bitcast.8, bf16[2048,512]{1,0:T(8,128)(2,1)} %bitcast.4, bf16[2048,128]{1,0:T(8,128)(2,1)} %bitcast.5), custom_call_target="tpu_custom_call" | custom-call | tf_op jit(solution)/shard_map/solve/pallas_call | solution.py:288
  86.0 50.1 %finish.1 = (f32[8,256,128]{2,1,0:T(8,128)}, f32[8,128]{1,0:T(8,128)}) custom-call(s32[320]{0:T(512)} %get-tuple-element.13.table_ref, bf16[8,256,512]{2,1,0:T(8,128)(2,1)} %get-tuple-element.14.picked_ref, bf16[8,256,128]{2,1,0:T(8,128)(2,1)} %a_ref.3, bf16[512,128]{1,0:T(8,128)(2,1)} %get-tuple-element.15.coef_ref, f32[8,128]{1,0:T(8,128)} %get-tuple-element.16.var_ref), custom_call_target="tpu_custom_call" | custom-call | tf_op jit(solution)/shard_map/finish/pallas_call | solution.py:451
  136.1 0.0 copy-start
  136.1 2.3 %copy.7 = f32[8,256,128]{2,1,0:T(8,128)} copy(f32[8,256,128]{2,1,0:T(8,128)} %get-tuple-element.22) | data formatting | bytes 2097152
  138.4 0.0 copy-done
  138.4 0.6 copy.8
Async XLA Ops:
  136.1 2.3 %copy-start = (f32[8,128]{1,0:T(8,128)S(1)}, f32[8,128]{1,0:T(8,128)}, u32[]{:S(2)}) copy-start(f32[8,128]{1,0:T(8,128)} %get-tuple-element.24) | copy-start | bytes 12292

commit v4 on v3

--- a/solution.py
+++ b/solution.py
@@ -19,6 +19,7 @@
 JUMP = 5
 VM = pl.BlockSpec(memory_space=pltpu.VMEM)
 SM = pl.BlockSpec(memory_space=pltpu.SMEM)
+HB = pl.BlockSpec(memory_space=pltpu.HBM)
 dma = pltpu.SemaphoreType.DMA
 
 SPREAD_SHORT, SPREAD_LONG = 11, 5
@@ -87,7 +88,7 @@
     return plan
 
 
-def spread_kernel(pred_ref, a_ref, picked_ref, theirs_ref, own_ref, *rest):
+def spread_kernel(pred_ref, a_ref, picked_hbm, theirs_ref, own_ref, picked_ref, keep, *rest):
     chunks = SPREAD_SHORT + SPREAD_LONG
     windows = rest[:chunks]
     relays = rest[chunks : chunks + SPREAD_LONG]
@@ -140,10 +141,12 @@
             for j in range(SLOTS):
                 picked_ref[k, span(u), j * R : (j + 1) * R] = windows[u][index[k * SLOTS + j]]
 
+    keep_own = pltpu.make_async_copy(a_ref.at[t], own_ref.at[t], keep.at[0])
+
     def copy_own():
         for u in range(chunks):
             windows[u][REACH * blocks :] = a_ref[:, span(u)]
-        own_ref[t] = a_ref[t]
+        keep_own.start()
 
     begun = False
     for is_long, c, r in listed_order(SPREAD_ORDER, SPREAD_SHORT):
@@ -162,7 +165,11 @@
             pick(u)
             for e in range(1, peers):
                 give(e, span(u)).start()
-    theirs_ref[t] = picked_ref[t]
+    keep_theirs = pltpu.make_async_copy(picked_ref.at[t], theirs_ref.at[t], keep.at[1])
+    keep_picked = pltpu.make_async_copy(picked_ref, picked_hbm, keep.at[2])
+    keep_theirs.start()
+    keep_picked.start()
+    keep_own.wait()
     for e in range(1, peers):
         give_own(e).wait_recv()
         give(e, slice(0, members)).wait_recv()
@@ -179,6 +186,8 @@
     for e in range(1, peers):
         give_own(e).wait_send()
         give(e, slice(0, members)).wait_send()
+    keep_theirs.wait()
+    keep_picked.wait()
 
 
 def spread(predecessors, anomalies, peers):
@@ -194,8 +203,9 @@
             jax.ShapeDtypeStruct((peers, members, R), bf16),
         ),
         in_specs=[SM, VM],
-        out_specs=(VM, VM, VM),
-        scratch_shapes=[pltpu.VMEM(((REACH + 1) * blocks, rows, R), bf16) for _ in range(chunks)]
+        out_specs=(HB, HB, HB),
+        scratch_shapes=[pltpu.VMEM((blocks, members, SLOTS * R), bf16), dma((3,))]
+        + [pltpu.VMEM(((REACH + 1) * blocks, rows, R), bf16) for _ in range(chunks)]
         + [pltpu.VMEM((JUMP - REACH, blocks, rows, R), bf16) for _ in range(SPREAD_LONG)]
         + [dma((REACH,)), dma((SPREAD_SHORT, REACH)), dma((JUMP,)), dma((SPREAD_LONG, JUMP))]
         + [dma((peers - 1,)) for _ in range(4)],
@@ -216,11 +226,14 @@
     def down(v, s):
         return jnp.broadcast_to(v[s : s + 1, :], (8, 128))
 
+    def columns(q):
+        return [across(rows[q], 8 * q + c) for c in range(8)]
+
+    t = columns(0)
     for q in range(groups):
         p = rows[q]
-        t = [across(p, 8 * q + c) for c in range(8)]
         for s in range(8):
-            inv = 1.0 / down(t[s], s)
+            inv = down(1.0 / t[s], s)
             at = lane == 8 * q + s
             row = jnp.where(at, inv, down(p, s) * inv)
             p = jnp.where(sub == s, row, jnp.where(at, 0.0, p) - t[s] * row)
@@ -229,14 +242,14 @@
                 t[c] = jnp.where(sub == s, n, t[c] - t[s] * n)
         b = [down(p, s) for s in range(8)]
         panel = (lane >= 8 * q) & (lane < 8 * q + 8)
-        for g in range(groups):
-            if g == q:
-                continue
+        for g in list(range(q + 1, groups)) + list(range(q)):
             old = rows[g]
-            new = jnp.where(panel, 0.0, old)
-            for s in range(8):
-                new = new - across(old, 8 * q + s) * b[s]
-            rows[g] = new
+            parts = [across(old, 8 * q + s) * b[s] for s in range(8)]
+            while len(parts) > 1:
+                parts = [x + y for x, y in zip(parts[::2], parts[1::2])]
+            rows[g] = jnp.where(panel, 0.0, old) - parts[0]
+            if g == q + 1:
+                t = columns(g)
         rows[q] = p
     return jnp.concatenate(rows, axis=0)
 
@@ -300,10 +313,12 @@
 
 
 def finish_kernel(
-    table_ref, picked_ref, a_ref, coef_ref, var_ref, out_ref, vars_ref,
-    all_ref, landed_vars, terms, short_landed, short_staged, long_landed, long_staged,
+    table_ref, picked_hbm, a_ref, coef_ref, var_ref, out_ref, vars_ref,
+    picked_ref, fetched, all_ref, landed_vars, terms, short_landed, short_staged, long_landed, long_staged,
     send, recv, var_send, var_recv, short_send, short_recv, long_send, long_recv,
 ):
+    fetch = pltpu.make_async_copy(picked_hbm, picked_ref, fetched)
+    fetch.start()
     p, n, t, peers, cores = places()
     blocks, members, _ = out_ref.shape
     chunks = COLLECT_SHORT + COLLECT_LONG
@@ -356,6 +371,7 @@
         for j in range(SLOTS):
             terms[k * SLOTS + j] = back[:, j * R : (j + 1) * R]
 
+    fetch.wait()
     weigh(t)
     for e in range(1, peers):
         variance(e).wait_recv()
@@ -454,9 +470,11 @@
             jax.ShapeDtypeStruct((blocks, members, R), f32),
             jax.ShapeDtypeStruct((blocks, R), f32),
         ),
-        in_specs=[SM, VM, VM, VM, VM],
+        in_specs=[SM, HB, VM, VM, VM],
         out_specs=(VM, VM),
         scratch_shapes=[
+            pltpu.VMEM(picked.shape, bf16),
+            dma,
             pltpu.VMEM((peers,) + coef.shape, bf16),
             pltpu.VMEM((peers,) + var.shape, f32),
             pltpu.VMEM((SLOTS * blocks + 1, members, R), f32),

time: 139 us -> 136 us (0.978)
  Pallas kernels: 135 us -> 133 us
    pallas_call x1, Pallas kernels: 62.1 us -> 60.1 us  [spread(): pl.pallas_call(spread_kernel, out_shape=(jax.ShapeDtypeStruct((blocks, me...]
where the time goes in v4:
time: 136 us
  Pallas kernels  133 us (98%)
  local copies, waits for them, and re-layouts  2.87 us (2%)
    pallas_call x1, Pallas kernels, spread(): pl.pallas_call(spread_kernel, out_shape=(jax.ShapeDtypeStruct((blocks, me...  60.1 us
    pallas_call x1, Pallas kernels, finish(): pl.pallas_call(finish_kernel, out_shape=(jax.ShapeDtypeStruct((blocks, me...  49.6 us
    pallas_call x1, Pallas kernels, solve(): pl.pallas_call(solve_kernel, out_shape=(jax.ShapeDtypeStruct((512, 128),...  22.8 us
    unnamed x4, local copies, waits for them, and re-layouts  2.87 us

profile of v4, /device:TPU:1, one launch (start us, length us, event | category | flops | bytes accessed | tf_op | source)
XLA Modules:
  0.0 136.1 jit_solution(655523870453616799)
XLA Ops:
  0.6 60.1 %spread.1 = (bf16[8,256,512]{2,1,0:T(8,128)(2,1)}, bf16[8,256,512]{2,1,0:T(8,128)(2,1)}, bf16[8,256,128]{2,1,0:T(8,128)(2,1)}) custom-call(s32[4,8]{1,0:T(4,128)} %bitcast.7, bf16[8,256,128]{2,1,0:T(8,128)(2,1)} %a_ref.3), custom_call_target="tpu_custom_call" | custom-call | tf_op jit(solution)/shard_map/spread/pallas_call | solution.py:198
  60.8 22.8 %solve.1 = (bf16[512,128]{1,0:T(8,128)(2,1)}, f32[8,128]{1,0:T(8,128)}, s32[320]{0:T(512)}) custom-call(s32[4,8]{1,0:T(4,128)} %bitcast.8, bf16[2048,512]{1,0:T(8,128)(2,1)} %bitcast.4, bf16[2048,128]{1,0:T(8,128)(2,1)} %bitcast.5), custom_call_target="tpu_custom_call" | custom-call | tf_op jit(solution)/shard_map/solve/pallas_call | solution.py:301
  83.6 49.6 %finish.1 = (f32[8,256,128]{2,1,0:T(8,128)}, f32[8,128]{1,0:T(8,128)}) custom-call(s32[320]{0:T(512)} %get-tuple-element.13.table_ref, bf16[8,256,512]{2,1,0:T(8,128)(2,1)} %get-tuple-element.14.picked_hbm, bf16[8,256,128]{2,1,0:T(8,128)(2,1)} %a_ref.3, bf16[512,128]{1,0:T(8,128)(2,1)} %get-tuple-element.15.coef_ref, f32[8,128]{1,0:T(8,128)} %get-tuple-element.16.var_ref), custom_call_target="tpu_custom_call" | custom-call | tf_op jit(solution)/shard_map/finish/pallas_call | solution.py:467
  133.2 0.0 copy-start
  133.2 2.3 %copy.7 = f32[8,256,128]{2,1,0:T(8,128)} copy(f32[8,256,128]{2,1,0:T(8,128)} %get-tuple-element.22) | data formatting | bytes 2097152
  135.5 0.0 copy-done
  135.5 0.6 copy.8
Async XLA Ops:
  133.2 2.3 %copy-start = (f32[8,128]{1,0:T(8,128)S(1)}, f32[8,128]{1,0:T(8,128)}, u32[]{:S(2)}) copy-start(f32[8,128]{1,0:T(8,128)} %get-tuple-element.24) | copy-start | bytes 12292
